TPU v7x, 8 devices: a whole 2x2x1 slice. The times are simulated.
8 devices in a mesh: dp: 1 (over z), tp: 8 (over y, x, core).
Axes of the slice: x: 2, y: 2, z: 1, core: 2. Of those that a mesh axis runs over, the one named last changes fastest.
Arguments:
- hidden: bfloat16 [16, 1536], P('dp')
- final_gain: bfloat16 [1536], replicated
- embed_table: bfloat16 [151936, 1536], P(None, 'tp')
- targets: int32 [16], P('dp')
- temperature: float32 [], replicated
Outputs:
- output 1: float32 [16], P('dp')
- output 2: float32 [16], P('dp')
- output 3: bfloat16 [16, 151936], P('dp', 'tp')
All inputs are finite; a program needn't handle non-finite values.
Results may differ from a plain program's by a relative error of at most 0.001.
Values sent between devices are 32-bit elements.
A program may use at most 1 GiB of HBM per device.

v0:
```python
import jax
import jax.numpy as jnp
from jax import lax
from jax.sharding import PartitionSpec as P

NORM_EPS = 1e-6


def solution(mesh):
    def local_scores(hidden, final_gain, table_cols, targets, value_a11):
        shard_index = lax.axis_index('tp')
        col_width = table_cols.shape[1]
        col_start = shard_index * col_width
        hidden_f32 = hidden.astype(jnp.float32)
        inv_rms = lax.rsqrt(jnp.mean(hidden_f32 * hidden_f32, axis=-1, keepdims=True) + NORM_EPS)
        hidden_cols = lax.dynamic_slice_in_dim(hidden, col_start, col_width, axis=1).astype(jnp.float32)
        gain_cols = lax.dynamic_slice_in_dim(final_gain, col_start, col_width).astype(jnp.float32)
        normed_cols = (hidden_cols * inv_rms * gain_cols).astype(jnp.bfloat16)
        partial_logits = lax.dot_general(normed_cols, table_cols, (((1,), (1,)), ((), ())),
                                         preferred_element_type=jnp.float32)
        logits = lax.psum_scatter(partial_logits, 'tp', scatter_dimension=1, tiled=True) / value_a11
        row_max = lax.pmax(jnp.max(logits, axis=-1), 'tp')
        shard_sum = jnp.sum(jnp.exp(logits - row_max[:, None]), axis=-1)
        log_norm = row_max + jnp.log(lax.psum(shard_sum, 'tp'))
        target_rows = jnp.take(table_cols, targets, axis=0)
        target_part = jnp.einsum('nd,nd->n', normed_cols, target_rows,
                                 preferred_element_type=jnp.float32)
        target_logit = lax.psum(target_part, 'tp') / value_a11
        token_probs = jnp.exp(logits - log_norm[:, None]).astype(jnp.bfloat16)
        return log_norm, target_logit - log_norm, token_probs

    return jax.shard_map(local_scores, mesh=mesh,
                         in_specs=(P('dp', None), P(None), P(None, 'tp'), P('dp'), P()),
                         out_specs=(P('dp'), P('dp'), P('dp', 'tp')),
                         check_vma=False)
```

profile of v0, /device:TPU:0, one launch (start us, length us, event | category | flops | bytes accessed | tf_op | source)
XLA Modules:
  0.0 227.3 jit_solution(9241316624760399181)
XLA Ops:
  7.2 0.0 all-reduce.4.cloned.1.call-start
  7.2 0.9 multiply_reduce_fusion
  8.1 0.8 dynamic-slice_convert_fusion
  8.9 24.7 %fusion.1 = f32[16,151936]{1,0:T(8,128)} fusion(bf16[151936,192]{0,1:T(8,128)(2,1)} %param.7, f32[192]{0:T(256)S(1)} %dynamic-slice_convert_fusion, f32[16]{0:T(128)S(1)} %add_rsqrt_fusion, bf16[16,1536]{1,0:T(8,128)(2,1)} %param.5, s32[]{:T(128)S(6)} %select_n.13), kind=kOutput, calls=%fused_computation.15 | convolution fusion | flops 933507072 | bytes 68076352 | tf_op jit(solution)/shard_map/dot_general | solution.py:19
  33.6 0.0 all-reduce.4.cloned.1.call-update
  33.6 0.0 copy-start.1
  33.6 81.7 %copy.9 = bf16[151936,192]{1,0:T(8,128)(2,1)} copy(bf16[151936,192]{0,1:T(8,128)(2,1)} %param.7) | data formatting | bytes 116686848 | tf_op args[2]
  116.0 0.0 copy-done.1
  116.0 1.3 gather_fusion
  117.3 49.3 %all-reduce.4.cloned.1.call-done = f32[16,151936]{1,0:T(8,128)} async-done(((f32[16,151936]{1,0:T(8,128)}), f32[16,151936]{1,0:T(8,128)}) %all-reduce.4.cloned.1.call-update) | async-done | bytes 9723920
  166.7 1.8 fusion.3
  168.4 0.9 fusion
  169.3 22.3 %pmax.7 = f32[16]{0:T(128)S(1)} all-reduce(f32[16]{0:T(128)S(1)} %fusion.3), channel_id=1, replica_groups=mesh['dp'=1,'tp'=8] {'tp'}, use_global_device_ids=true, to_apply=%region_3.0 | all-reduce | flops 16 | bytes 128 | tf_op jit(solution)/shard_map/pmax | solution.py:22
  191.6 1.8 exponential_reduce_fusion
  193.4 24.0 %all-reduce.1 = (f32[16]{0:T(128)S(1)}, f32[16]{0:T(128)S(1)}) all-reduce(f32[16]{0:T(128)S(1)} %exponential_reduce_fusion, f32[16]{0:T(128)S(1)} %fusion), channel_id=1, replica_groups=mesh['dp'=1,'tp'=8] {'tp'}, use_global_device_ids=true, to_apply=%region_5.0 | all-reduce | flops 32 | bytes 256 | tf_op jit(solution)/shard_map/psum | solution.py:24
  217.4 0.5 divide_subtract_fusion
  217.9 0.0 copy-start
  217.9 2.5 %exponential_convert_fusion = bf16[16,18992]{1,0:T(8,128)(2,1)} fusion(f32[16]{0:T(128)S(1)} %get-tuple-element.6, f32[]{:T(128)S(6)} %copy.18, f32[16,151936]{1,0:T(8,128)} %all-reduce.4.cloned.1.call-done, u32[]{:T(128)S(6)} %multiply.8), kind=kLoop, calls=%fused_computation.2 | loop fusion | flops 911616 | bytes 1823304 | tf_op jit(solution)/shard_map/convert_element_type | solution.py:29
  220.4 0.0 copy-done
  (4 shorter events, 0.0 us)
Async XLA Ops:
  7.2 159.5 %all-reduce.4.cloned.1.call-start = ((), (), s32[]{:S(2)}) async-start(), calls=%async_computation | async-start | bytes 19447808
  33.6 82.4 %copy-start.1 = (s32[16]{0:T(128)S(1)}, s32[16]{0:T(128)}, u32[]{:S(2)}) copy-start(s32[16]{0:T(128)} %param.8) | copy-start | bytes 196
  217.9 2.5 %copy-start = (f32[16]{0:T(128)}, f32[16]{0:T(128)S(1)}, u32[]{:S(2)}) copy-start(f32[16]{0:T(128)S(1)} %get-tuple-element.6) | copy-start | bytes 196
Sparse Core Ops, SparseCore 0:
  33.7 132.8 all-reduce.3
where the time goes:
time: 230 us; the launch traced here: 227 us
  local copies, waits for them, and re-layouts  83 us (36%)
  waiting for transfers between devices  49.4 us (21%)
  blocking collectives  46.3 us (20%)
  matrix products  24.7 us (11%)
  between operations  14.7 us (6%)
  other arithmetic  9.2 us (4%)
    unnamed x5, local copies, waits for them, and re-layouts  81.7 us
    unnamed x2, waiting for transfers between devices  49.4 us
    dot_general x1, matrix products, local_scores(): lax.dot_general(normed_cols, table_cols, (((1,), (1,)), ((), ())), prefer...  24.7 us
    psum x1, blocking collectives, local_scores(): log_norm = row_max + jnp.log(lax.psum(shard_sum, 'tp'))  24 us
    pmax x1, blocking collectives, local_scores(): row_max = lax.pmax(jnp.max(logits, axis=-1), 'tp')  22.3 us
  transfers between devices with their start and end apart: 1, of which 1 were waited for; matrix products, arithmetic and copies ran while one was open for 37% of the time, Pallas kernels for 0%

commit v1 on v0

v1 whole, which is shorter than its diff:
```python
import jax
import jax.numpy as jnp
from jax import lax
from jax.experimental import pallas as pl
from jax.experimental.pallas import tpu as pltpu
from jax.sharding import PartitionSpec as P

NORM_EPS = 1e-6
LANES = 128
LANE_CHUNKS = 5
DEPTH = 4
NEG = -3.0e38
MESH = pl.DeviceIdType.MESH


def _kernel(shape, hid_hbm, gain_hbm, table_hbm, tgt_hbm, temp_hbm, logits_ref, stats_ref,
            hid, gain, tgt, temp, normed, tbuf, psend, prec, own, r1, r2, mine, every,
            in_sem, tsem, d2d_ssem, d2d_rsem, s1_ssem, s1_rsem, s2_ssem, s2_rsem, st_ssem, st_rsem):
    vocab, rows_per, tokens, width, tiles, chunk = shape
    half_tiles = tiles // 2
    nl = LANE_CHUNKS
    steps = 4 * nl
    me = lax.axis_index('tp')
    core, mx, my = me % 2, (me // 2) % 2, me // 4
    partner = me + 1 - 2 * core
    xn = me + 2 - 4 * mx
    yn = me + 4 - 8 * my
    first = (xn, yn)
    second = (yn, xn)

    def region_tile(d):
        return (d * rows_per) // LANES - d // 7

    def table_copy(i, q):
        p, j = i // nl, i % nl
        lane = q % 2
        a, b = 1 - p // 2, 1 - p % 2
        fx, fy = (a, b) if lane == 0 else (b, a)
        k = 1 - core if q < 2 else core
        d = (my + fy * (1 - 2 * my)) * 4 + (mx + fx * (1 - 2 * mx)) * 2 + k
        tile = region_tile(d) + lane * half_tiles + j * (chunk // LANES)
        col = pl.multiple_of(tile * LANES, LANES)
        slot = (i % DEPTH) * 4 + q
        return pltpu.make_async_copy(table_hbm.at[:, pl.ds(col, chunk)], tbuf.at[slot], tsem.at[slot])

    for i in range(DEPTH):
        for q in range(4):
            if i == 0 and q == 2:
                pltpu.make_async_copy(hid_hbm, hid, in_sem.at[0]).start()
                pltpu.make_async_copy(gain_hbm, gain, in_sem.at[1]).start()
            table_copy(i, q).start()
    pltpu.make_async_copy(tgt_hbm, tgt, in_sem.at[2]).start()
    pltpu.make_async_copy(temp_hbm, temp, in_sem.at[3]).start()

    barrier = pltpu.get_barrier_semaphore()
    for r in range(1, 8):
        pl.semaphore_signal(barrier, inc=1, device_id={'tp': (me + r) % 8}, device_id_type=MESH)

    pltpu.make_async_copy(hid_hbm, hid, in_sem.at[0]).wait()
    pltpu.make_async_copy(gain_hbm, gain, in_sem.at[1]).wait()
    h = hid[...].astype(jnp.float32)
    inv_rms = lax.rsqrt(jnp.mean(h * h, axis=-1, keepdims=True) + NORM_EPS)
    col0 = pl.multiple_of(((me * 3) // 2) * LANES, LANES)
    hc = hid[:, pl.ds(col0, 2 * LANES)].astype(jnp.float32)
    gc = gain[:, pl.ds(col0, 2 * LANES)].astype(jnp.float32)
    u = hc * inv_rms * gc
    u = jnp.where(core == 0, u[:, :width], u[:, 2 * LANES - width:])
    normed[...] = u.astype(jnp.bfloat16)

    pl.semaphore_wait(barrier, 7)

    def d2d(s):
        return pltpu.make_async_remote_copy(
            src_ref=psend.at[s], dst_ref=prec.at[s], send_sem=d2d_ssem.at[s], recv_sem=d2d_rsem.at[s],
            device_id={'tp': partner}, device_id_type=MESH)

    def stage1(lane, i):
        s = i * 2 + lane
        return pltpu.make_async_remote_copy(
            src_ref=own.at[s], dst_ref=r1.at[s], send_sem=s1_ssem.at[s], recv_sem=s1_rsem.at[s],
            device_id={'tp': first[lane]}, device_id_type=MESH)

    def stage2(lane, j):
        s = j * 2 + lane
        return pltpu.make_async_remote_copy(
            src_ref=own.at[4 * nl + s], dst_ref=r2.at[s], send_sem=s2_ssem.at[s], recv_sem=s2_rsem.at[s],
            device_id={'tp': second[lane]}, device_id_type=MESH)

    def compute(i, prefetch):
        for q in range(4):
            s = i * 2 + q % 2
            slot = (i % DEPTH) * 4 + q
            table_copy(i, q).wait()
            out = psend if q < 2 else own
            out[s] = jnp.dot(normed[...], tbuf[slot], preferred_element_type=jnp.float32)
            if q < 2:
                d2d(s).start()
            if prefetch:
                table_copy(i + DEPTH, q).start()

    def gather_pair(i, send):
        for lane in range(2):
            s = i * 2 + lane
            d2d(s).wait_recv()
            own[s] = own[s] + prec[s]
            if send:
                stage1(lane, i).start()

    compute(0, True)

    def loop_send(i, carry):
        compute(i, True)
        gather_pair(i - 1, True)
        return carry

    def loop_keep(i, carry):
        compute(i, True)
        gather_pair(i - 1, False)
        return carry

    def loop_last(i, carry):
        compute(i, False)
        gather_pair(i - 1, False)
        return carry

    lax.fori_loop(1, 2 * nl + 1, loop_send, 0)
    lax.fori_loop(2 * nl + 1, steps - DEPTH, loop_keep, 0)
    lax.fori_loop(steps - DEPTH, steps, loop_last, 0)
    gather_pair(steps - 1, False)

    def forward(j, carry):
        for lane in range(2):
            stage1(lane, j).wait_recv()
            s = (2 * nl + j) * 2 + lane
            own[s] = own[s] + r1[j * 2 + lane]
            stage2(lane, j).start()
        return carry

    lax.fori_loop(0, nl, forward, 0)

    pltpu.make_async_copy(tgt_hbm, tgt, in_sem.at[2]).wait()
    pltpu.make_async_copy(temp_hbm, temp, in_sem.at[3]).wait()
    temperature = temp[0]
    row = lax.broadcasted_iota(jnp.int32, (tokens, LANES), 0)
    lane_id = lax.broadcasted_iota(jnp.int32, (tokens, LANES), 1)
    target = jnp.zeros((tokens, LANES), jnp.int32)
    for t in range(tokens):
        target = jnp.where(row == t, tgt[t], target)
    lo = me * rows_per
    base = region_tile(me) * LANES

    def finish(j, carry):
        m, total, picked = carry
        for lane in range(2):
            stage1(lane, nl + j).wait_recv()
            stage2(lane, j).wait_recv()
            z = own[(3 * nl + j) * 2 + lane] + r1[(nl + j) * 2 + lane] + r2[j * 2 + lane]
            t = z / temperature
            off = pl.multiple_of((lane * half_tiles + j * (chunk // LANES)) * LANES, LANES)
            logits_ref[:, pl.ds(off, chunk)] = t
            parts = []
            top = m
            for k in range(chunk // LANES):
                piece = t[:, k * LANES:(k + 1) * LANES]
                col = lane_id + (base + off + k * LANES)
                inside = (col >= lo) & (col < lo + rows_per)
                piece_in = jnp.where(inside, piece, NEG)
                picked = picked + jnp.where(inside & (col == target), piece, 0.0)
                parts.append(piece_in)
                top = jnp.maximum(top, piece_in)
            total = total * jnp.exp(m - top)
            for piece_in in parts:
                total = total + jnp.exp(piece_in - top)
            m = top
        return m, total, picked

    m, total, picked = lax.fori_loop(
        0, nl, finish,
        (jnp.full((tokens, LANES), NEG, jnp.float32), jnp.zeros((tokens, LANES), jnp.float32),
         jnp.zeros((tokens, LANES), jnp.float32)))
    m_row = jnp.max(m, axis=-1, keepdims=True)
    s_row = jnp.sum(total * jnp.exp(m - m_row), axis=-1, keepdims=True)
    p_row = jnp.sum(picked, axis=-1, keepdims=True)
    packed = jnp.where(lane_id == 0, m_row, jnp.where(lane_id == 1, s_row, p_row))
    mine[...] = packed

    def share(peer, slot):
        return pltpu.make_async_remote_copy(
            src_ref=mine, dst_ref=every.at[slot], send_sem=st_ssem.at[peer], recv_sem=st_rsem.at[slot],
            device_id={'tp': peer}, device_id_type=MESH)

    peers = [(me + r) % 8 for r in (4, 3, 5, 2, 6, 1, 7)]
    for peer in peers:
        share(peer, me).start()
    blocks = [packed]
    for peer in peers:
        share(peer, peer).wait_recv()
        blocks.append(every[peer])
    ms = [b[:, 0:1] for b in blocks]
    m_all = ms[0]
    for v in ms[1:]:
        m_all = jnp.maximum(m_all, v)
    s_all = jnp.zeros_like(m_all)
    p_all = jnp.zeros_like(m_all)
    for b in blocks:
        s_all = s_all + b[:, 1:2] * jnp.exp(b[:, 0:1] - m_all)
        p_all = p_all + b[:, 2:3]
    log_norm = m_all + jnp.log(s_all)
    stats_ref[...] = jnp.where(lane_id == 0, log_norm, p_all - log_norm)

    def drain(s, carry):
        d2d(s).wait_send()
        return carry
    lax.fori_loop(0, 2 * steps, drain, 0)

    def drain1(i, carry):
        for lane in range(2):
            stage1(lane, i).wait_send()
        return carry
    lax.fori_loop(0, 2 * nl, drain1, 0)

    def drain2(j, carry):
        for lane in range(2):
            stage2(lane, j).wait_send()
        return carry
    lax.fori_loop(0, nl, drain2, 0)
    for peer in peers:
        share(peer, me).wait_send()


def _scores(hidden, gain, table, targets, temperature):
    tokens, hidden_dim = hidden.shape
    vocab, width = table.shape
    rows_per = vocab // 8
    nl = LANE_CHUNKS
    unit = 2 * nl
    need = -(-rows_per // LANES) + 1
    tiles = -(-need // unit) * unit
    chunk = tiles // unit * LANES
    steps = 4 * nl
    f32 = jnp.float32
    dma = pltpu.SemaphoreType.DMA
    block = (tokens, chunk)
    return pl.pallas_call(
        lambda *refs: _kernel((vocab, rows_per, tokens, width, tiles, chunk), *refs),
        out_shape=(jax.ShapeDtypeStruct((tokens, tiles * LANES), f32),
                   jax.ShapeDtypeStruct((tokens, LANES), f32)),
        in_specs=[pl.BlockSpec(memory_space=pltpu.HBM)] * 5,
        out_specs=(pl.BlockSpec(memory_space=pltpu.VMEM), pl.BlockSpec(memory_space=pltpu.VMEM)),
        scratch_shapes=[
            pltpu.VMEM((tokens, hidden_dim), jnp.bfloat16),
            pltpu.VMEM((1, hidden_dim), jnp.bfloat16),
            pltpu.SMEM((tokens,), jnp.int32),
            pltpu.SMEM((1,), f32),
            pltpu.VMEM((tokens, width), jnp.bfloat16),
            pltpu.VMEM((DEPTH * 4, width, chunk), jnp.bfloat16),
            pltpu.VMEM((2 * steps,) + block, f32),
            pltpu.VMEM((2 * steps,) + block, f32),
            pltpu.VMEM((2 * steps,) + block, f32),
            pltpu.VMEM((4 * nl,) + block, f32),
            pltpu.VMEM((2 * nl,) + block, f32),
            pltpu.VMEM((tokens, LANES), f32),
            pltpu.VMEM((8, tokens, LANES), f32),
            dma((4,)), dma((DEPTH * 4,)),
            dma((2 * steps,)), dma((2 * steps,)),
            dma((4 * nl,)), dma((4 * nl,)),
            dma((2 * nl,)), dma((2 * nl,)),
            dma((8,)), dma((8,)),
        ],
        compiler_params=pltpu.CompilerParams(collective_id=0, has_side_effects=True,
                                             vmem_limit_bytes=67043328),
        name='head',
    )(hidden, gain.reshape(1, -1), table.T, targets, temperature.reshape(1))


def solution(mesh):
    def local_scores(hidden, final_gain, table_cols, targets, temperature):
        rows_per = table_cols.shape[0] // 8
        me = lax.axis_index('tp')
        logits, stats = _scores(hidden, final_gain, table_cols, targets, temperature)
        start = me * rows_per - ((me * rows_per) // LANES - me // 7) * LANES
        part = lax.dynamic_slice_in_dim(logits, start, rows_per, axis=1)
        log_norm = stats[:, 0]
        token_probs = jnp.exp(part - stats[:, 0:1]).astype(jnp.bfloat16)
        return log_norm, stats[:, 1], token_probs

    return jax.shard_map(local_scores, mesh=mesh,
                         in_specs=(P('dp', None), P(None), P(None, 'tp'), P('dp'), P()),
                         out_specs=(P('dp'), P('dp'), P('dp', 'tp')),
                         check_vma=False)
```

time: 230 us -> 63 us (0.27); the launches traced: 227 us -> 62.7 us
  local copies, waits for them, and re-layouts: 83 us -> 2.76 us
  Pallas kernels: 0 us -> 56.2 us
  waiting for transfers between devices: 49.4 us -> 0 us
  blocking collectives: 46.3 us -> 0 us
  matrix products: 24.7 us -> 0 us
  between operations: 14.7 us -> 1.29 us
  other arithmetic: 9.2 us -> 2.5 us
    unnamed x5 -> x2, local copies, waits for them, and re-layouts: 81.7 us -> 0.01 us
    pallas_call x0 -> x1, Pallas kernels: none -> 56.2 us  [_scores(): pl.pallas_call(lambda *refs: _kernel((vocab, rows_per, tokens, width, til...]
    unnamed x2 -> x0, waiting for transfers between devices: 49.4 us -> none
    dot_general x1 -> x0, matrix products: 24.7 us -> none  [local_scores(): lax.dot_general(normed_cols, table_cols, (((1,), (1,)), ((), ())), prefer...]
    psum x1 -> x0, blocking collectives: 24 us -> none  [local_scores(): log_norm = row_max + jnp.log(lax.psum(shard_sum, 'tp'))]
    pmax x1 -> x0, blocking collectives: 22.3 us -> none  [local_scores(): row_max = lax.pmax(jnp.max(logits, axis=-1), 'tp')]
    reduce_sum x2 -> x0, other arithmetic: 2.71 us -> none  [the longest x1 1.78 us: local_scores(): shard_sum = jnp.sum(jnp.exp(logits - row_max[:, None]), axis=-1)]
  transfers between devices with their start and end apart: 1 -> 0, of which waited for: 1 -> 0; matrix products, arithmetic and copies ran while one was open for 37% -> 0% of each run, Pallas kernels for 0% -> 0%
where the time goes in v1:
time: 63 us; the launch traced here: 62.7 us
  Pallas kernels  56.2 us (89%)
  local copies, waits for them, and re-layouts  2.76 us (4%)
  other arithmetic  2.5 us (4%)
  between operations  1.29 us (2%)
    pallas_call x1, Pallas kernels, _scores(): pl.pallas_call(lambda *refs: _kernel((vocab, rows_per, tokens, width, til...  56.2 us
    convert_element_type x1, other arithmetic, local_scores(): token_probs = jnp.exp(part - stats[:, 0:1]).astype(jnp.bfloat16)  2.5 us
    slice x1, local copies, waits for them, and re-layouts, local_scores(): return (log_norm, stats[:, 1], token_probs)  1.47 us
    reshape x1, local copies, waits for them, and re-layouts, _scores(): gain.reshape(1, -1)  1.29 us

profile of v1, /device:TPU:0, one launch (start us, length us, event | category | flops | bytes accessed | tf_op | source)
XLA Modules:
  0.0 62.7 jit_solution(388425607491523500)
XLA Ops:
  0.6 1.3 %reshape.12.refs_1_ = bf16[1,1536]{1,0:T(2,128)(2,1)} reshape(bf16[1536]{0:T(1024)(128)(2,1)} %param.6) | data formatting | bytes 6144 | tf_op jit(solution)/shard_map/reshape | solution.py:273
  2.6 56.2 %head.1 = (f32[16,19200]{1,0:T(8,128)}, f32[16,128]{1,0:T(8,128)}) custom-call(bf16[16,1536]{1,0:T(8,128)(2,1)} %refs_0_.1, bf16[1,1536]{1,0:T(2,128)(2,1)} %reshape.12.refs_1_, bf16[192,151936]{1,0:T(8,128)(2,1)} %bitcast.3, s32[16]{0:T(128)} %refs_3_.1, f32[1]{0:T(128)} %bitcast.2.refs_4_), custom_call_target="tpu_custom_call" | custom-call | tf_op jit(solution)/shard_map/head/pallas_call | solution.py:244
  58.7 1.5 %slice_reduce_fusion = (f32[16]{0:T(128)}, f32[16]{0:T(128)S(1)}) fusion(f32[16,128]{1,0:T(8,128)} %get-tuple-element.5), kind=kLoop, calls=%fused_computation.1 | loop fusion | bytes 256 | tf_op jit(solution)/shard_map/slice | solution.py:285
  60.2 0.0 copy-start
  60.2 2.5 %exponential_convert_fusion = bf16[16,18992]{1,0:T(8,128)(2,1)} fusion(f32[16,19200]{1,0:T(8,128)} %get-tuple-element.6, s32[]{:T(128)S(6)} %select_n.13, f32[16]{0:T(128)S(1)} %get-tuple-element.8), kind=kLoop, calls=%fused_computation | loop fusion | flops 607744 | bytes 1823300 | tf_op jit(solution)/shard_map/convert_element_type | solution.py:284
  62.7 0.0 copy-done
Async XLA Ops:
  60.2 2.5 %copy-start = (f32[16]{0:T(128)}, f32[16]{0:T(128)S(1)}, u32[]{:S(2)}) copy-start(f32[16]{0:T(128)S(1)} %get-tuple-element.8) | copy-start | bytes 196

commit v2 on v1

v2 whole, which is shorter than its diff:
```python
import jax
import jax.numpy as jnp
from jax import lax
from jax.experimental import pallas as pl
from jax.experimental.pallas import tpu as pltpu
from jax.sharding import PartitionSpec as P

NORM_EPS = 1e-6
LANES = 128
LANE_CHUNKS = 5
DEPTH = 4
NEG = -3.0e38
MESH = pl.DeviceIdType.MESH


def _kernel(shape, hid_hbm, gain_hbm, table_hbm, tgt_hbm, temp, probs_ref, ln_ref, tl_ref,
            hid, gain, gain32, tgt, normed, tbuf, psend, prec, own, r1, r2, logits, shifted, mine, every,
            in_sem, tsem, d2d_ssem, d2d_rsem, s1_ssem, s1_rsem, s2_ssem, s2_rsem, st_ssem, st_rsem):
    rows_per, tokens, width, tiles, chunk = shape
    half_tiles = tiles // 2
    nl = LANE_CHUNKS
    steps = 4 * nl
    me = lax.axis_index('tp')
    core, mx, my = me % 2, (me // 2) % 2, me // 4
    partner = me + 1 - 2 * core
    xn = me + 2 - 4 * mx
    yn = me + 4 - 8 * my
    first = (xn, yn)
    second = (yn, xn)

    def region_tile(d):
        return (d * rows_per) // LANES - d // 7

    def table_copy(i, q):
        p, j = i // nl, i % nl
        lane = q % 2
        a, b = 1 - p // 2, 1 - p % 2
        fx, fy = (a, b) if lane == 0 else (b, a)
        k = 1 - core if q < 2 else core
        d = (my + fy * (1 - 2 * my)) * 4 + (mx + fx * (1 - 2 * mx)) * 2 + k
        tile = region_tile(d) + lane * half_tiles + j * (chunk // LANES)
        col = pl.multiple_of(tile * LANES, LANES)
        slot = (i % DEPTH) * 4 + q
        return pltpu.make_async_copy(table_hbm.at[:, pl.ds(col, chunk)], tbuf.at[slot], tsem.at[slot])

    small = [pltpu.make_async_copy(src, dst, in_sem.at[n]) for n, (src, dst) in enumerate(
        ((hid_hbm, hid), (gain_hbm, gain), (tgt_hbm, tgt)))]
    small[0].start()
    small[1].start()
    for q in range(4):
        table_copy(0, q).start()

    barrier = pltpu.get_barrier_semaphore()
    for r in range(1, 8):
        pl.semaphore_signal(barrier, inc=1, device_id={'tp': (me + r) % 8}, device_id_type=MESH)

    small[0].wait()
    small[1].wait()
    h = hid[...].astype(jnp.float32)
    inv_rms = lax.rsqrt(jnp.mean(h * h, axis=-1, keepdims=True) + NORM_EPS)
    gain32[...] = gain[...].astype(jnp.float32)
    g0 = (me * 3) // 2
    hc = hid[:, pl.ds(pl.multiple_of(g0 * LANES, LANES), 2 * LANES)].astype(jnp.float32)
    u0 = hc[:, :LANES] * inv_rms * gain32[pl.ds(g0, 1), :]
    u1 = hc[:, LANES:] * inv_rms * gain32[pl.ds(g0 + 1, 1), :]
    u = jnp.concatenate([u0, u1], axis=1)
    u = jnp.where(core == 0, u[:, :width], u[:, 2 * LANES - width:])
    normed[...] = u.astype(jnp.bfloat16)

    for i in range(1, DEPTH):
        for q in range(4):
            table_copy(i, q).start()
    small[2].start()

    pl.semaphore_wait(barrier, 7)

    def d2d(s):
        return pltpu.make_async_remote_copy(
            src_ref=psend.at[s], dst_ref=prec.at[s], send_sem=d2d_ssem.at[s], recv_sem=d2d_rsem.at[s],
            device_id={'tp': partner}, device_id_type=MESH)

    def stage1(lane, i):
        s = i * 2 + lane
        return pltpu.make_async_remote_copy(
            src_ref=own.at[s], dst_ref=r1.at[s], send_sem=s1_ssem.at[s], recv_sem=s1_rsem.at[s],
            device_id={'tp': first[lane]}, device_id_type=MESH)

    def stage2(lane, j):
        s = j * 2 + lane
        return pltpu.make_async_remote_copy(
            src_ref=own.at[4 * nl + s], dst_ref=r2.at[s], send_sem=s2_ssem.at[s], recv_sem=s2_rsem.at[s],
            device_id={'tp': second[lane]}, device_id_type=MESH)

    def compute(i, qs, prefetch):
        for q in qs:
            s = i * 2 + q % 2
            slot = (i % DEPTH) * 4 + q
            table_copy(i, q).wait()
            out = psend if q < 2 else own
            out[s] = jnp.dot(normed[...], tbuf[slot], preferred_element_type=jnp.float32)
            if q < 2:
                d2d(s).start()
            if prefetch is None:
                @pl.when(i + DEPTH < steps)
                def _():
                    table_copy(i + DEPTH, q).start()
            elif prefetch:
                table_copy(i + DEPTH, q).start()

    theirs, ours = (0, 1), (2, 3)

    def gather_pair(i, send):
        for lane in range(2):
            s = i * 2 + lane
            d2d(s).wait_recv()
            own[s] = own[s] + prec[s]
            if send:
                stage1(lane, i).start()

    compute(0, theirs, True)
    compute(0, ours, True)
    compute(1, theirs, True)

    def loop_send(i, carry):
        gather_pair(i, True)
        compute(i + 1, ours, True)
        compute(i + 2, theirs, True)
        return carry

    def loop_keep(i, carry):
        gather_pair(i, False)
        compute(i + 1, ours, None)
        compute(i + 2, theirs, None)
        return carry

    lax.fori_loop(0, 2 * nl, loop_send, 0)
    lax.fori_loop(2 * nl, steps - 2, loop_keep, 0)
    gather_pair(steps - 2, False)
    compute(steps - 1, ours, False)
    gather_pair(steps - 1, False)

    def forward(j, carry):
        for lane in range(2):
            stage1(lane, j).wait_recv()
            s = (2 * nl + j) * 2 + lane
            own[s] = own[s] + r1[j * 2 + lane]
            stage2(lane, j).start()
        return carry

    lax.fori_loop(0, nl, forward, 0)

    small[2].wait()
    temperature = temp[0]
    row = lax.broadcasted_iota(jnp.int32, (tokens, LANES), 0)
    lane_id = lax.broadcasted_iota(jnp.int32, (tokens, LANES), 1)
    target = jnp.zeros((tokens, LANES), jnp.int32)
    for t in range(tokens):
        target = jnp.where(row == t, tgt[t], target)
    lo = me * rows_per
    base = region_tile(me) * LANES

    def finish(j, carry):
        m, total, picked = carry
        for lane in range(2):
            stage1(lane, nl + j).wait_recv()
            stage2(lane, j).wait_recv()
            z = own[(3 * nl + j) * 2 + lane] + r1[(nl + j) * 2 + lane] + r2[j * 2 + lane]
            t = z / temperature
            off = pl.multiple_of((lane * half_tiles + j * (chunk // LANES)) * LANES, LANES)
            logits[:, pl.ds(off, chunk)] = t
            parts = []
            top = m
            for k in range(chunk // LANES):
                piece = t[:, k * LANES:(k + 1) * LANES]
                col = lane_id + (base + off + k * LANES)
                inside = (col >= lo) & (col < lo + rows_per)
                piece_in = jnp.where(inside, piece, NEG)
                picked = picked + jnp.where(inside & (col == target), piece, 0.0)
                parts.append(piece_in)
                top = jnp.maximum(top, piece_in)
            total = total * jnp.exp(m - top)
            for piece_in in parts:
                total = total + jnp.exp(piece_in - top)
            m = top
        return m, total, picked

    m, total, picked = lax.fori_loop(
        0, nl, finish,
        (jnp.full((tokens, LANES), NEG, jnp.float32), jnp.zeros((tokens, LANES), jnp.float32),
         jnp.zeros((tokens, LANES), jnp.float32)))
    m_row = jnp.max(m, axis=-1, keepdims=True)
    s_row = jnp.sum(total * jnp.exp(m - m_row), axis=-1, keepdims=True)
    p_row = jnp.sum(picked, axis=-1, keepdims=True)
    hs = tokens // 2
    lane8 = lax.broadcasted_iota(jnp.int32, (hs, LANES), 1)
    packed = jnp.broadcast_to(p_row[hs:], (hs, LANES))
    for n, v in enumerate((m_row[:hs], m_row[hs:], s_row[:hs], s_row[hs:], p_row[:hs])):
        packed = jnp.where(lane8 == n, v, packed)
    mine[...] = packed

    def share(peer, slot):
        return pltpu.make_async_remote_copy(
            src_ref=mine, dst_ref=every.at[slot], send_sem=st_ssem.at[peer], recv_sem=st_rsem.at[slot],
            device_id={'tp': peer}, device_id_type=MESH)

    far = me + 6 - 4 * mx - 8 * my + 0 * core
    peers = [far, far + 1 - 2 * core, yn, yn + 1 - 2 * core, xn, xn + 1 - 2 * core, partner]
    for peer in peers:
        share(peer, me).start()

    shift = lo - base
    skip, turn = shift // LANES, shift % LANES
    rot = (LANES - turn) % LANES
    out_tiles = -(-rows_per // LANES)
    keep = lane_id < LANES - turn

    def turned(k):
        at = pl.multiple_of((skip + k) * LANES, LANES)
        return pltpu.roll(logits[:, pl.ds(at, LANES)], rot, axis=1)

    cur = turned(0)
    for k in range(out_tiles):
        if k + 1 < out_tiles:
            nxt = turned(k + 1)
        else:
            nxt = pltpu.roll(logits[:, (tiles - 1) * LANES:tiles * LANES], rot, axis=1)
        shifted[:, k * LANES:(k + 1) * LANES] = jnp.where(keep, cur, nxt)
        cur = nxt

    def drain(s, carry):
        d2d(s).wait_send()
        return carry
    lax.fori_loop(0, 2 * steps, drain, 0)

    def drain1(i, carry):
        for lane in range(2):
            stage1(lane, i).wait_send()
        return carry
    lax.fori_loop(0, 2 * nl, drain1, 0)

    def drain2(j, carry):
        for lane in range(2):
            stage2(lane, j).wait_send()
        return carry
    lax.fori_loop(0, nl, drain2, 0)

    blocks = [packed]
    for peer in reversed(peers):
        share(peer, peer).wait_recv()
        blocks.append(every[peer])

    def rows16(n):
        return [jnp.concatenate([b[:, n:n + 1], b[:, n + 1:n + 2]], axis=0) for b in blocks]

    ms, ss, ps = rows16(0), rows16(2), rows16(4)
    m_all = ms[0]
    for v in ms[1:]:
        m_all = jnp.maximum(m_all, v)
    s_all = jnp.zeros_like(m_all)
    p_all = jnp.zeros_like(m_all)
    for mv, sv, pv in zip(ms, ss, ps):
        s_all = s_all + sv * jnp.exp(mv - m_all)
        p_all = p_all + pv
    log_norm = m_all + jnp.log(s_all)

    step = 19 * LANES
    for at in range(0, rows_per, step):
        end = min(at + step, rows_per)
        probs_ref[:, at:end] = jnp.exp(shifted[:, at:end] - log_norm).astype(jnp.bfloat16)

    def as_row(v):
        spread = jnp.where(lane_id == row, jnp.broadcast_to(v, (tokens, LANES)), 0.0)
        return jnp.sum(spread, axis=0, keepdims=True)[:, :tokens]
    ln_ref[...] = as_row(log_norm)
    tl_ref[...] = as_row(p_all - log_norm)
    for peer in peers:
        share(peer, me).wait_send()


def _scores(hidden, gain, table, targets, temperature):
    tokens, hidden_dim = hidden.shape
    vocab, width = table.shape
    rows_per = vocab // 8
    nl = LANE_CHUNKS
    unit = 2 * nl
    need = -(-rows_per // LANES) + 1
    tiles = -(-need // unit) * unit
    chunk = tiles // unit * LANES
    steps = 4 * nl
    out_tiles = -(-rows_per // LANES)
    f32 = jnp.float32
    dma = pltpu.SemaphoreType.DMA
    block = (tokens, chunk)
    grows = hidden_dim // LANES
    hbm = lambda v: pltpu.with_memory_space_constraint(v, pltpu.HBM)
    return pl.pallas_call(
        lambda *refs: _kernel((rows_per, tokens, width, tiles, chunk), *refs),
        out_shape=(pltpu.VMEM((tokens, rows_per), jnp.bfloat16),
                   pltpu.VMEM((1, tokens), f32), pltpu.VMEM((1, tokens), f32)),
        in_specs=[pl.BlockSpec(memory_space=pltpu.HBM)] * 4 + [pl.BlockSpec(memory_space=pltpu.SMEM)],
        out_specs=(pl.BlockSpec(memory_space=pltpu.VMEM),) * 3,
        scratch_shapes=[
            pltpu.VMEM((tokens, hidden_dim), jnp.bfloat16),
            pltpu.VMEM((grows, LANES), jnp.bfloat16),
            pltpu.VMEM((grows, LANES), f32),
            pltpu.SMEM((tokens,), jnp.int32),
            pltpu.VMEM((tokens, width), jnp.bfloat16),
            pltpu.VMEM((DEPTH * 4, width, chunk), jnp.bfloat16),
            pltpu.VMEM((2 * steps,) + block, f32),
            pltpu.VMEM((2 * steps,) + block, f32),
            pltpu.VMEM((2 * steps,) + block, f32),
            pltpu.VMEM((4 * nl,) + block, f32),
            pltpu.VMEM((2 * nl,) + block, f32),
            pltpu.VMEM((tokens, tiles * LANES), f32),
            pltpu.VMEM((tokens, out_tiles * LANES), f32),
            pltpu.VMEM((tokens // 2, LANES), f32),
            pltpu.VMEM((8, tokens // 2, LANES), f32),
            dma((3,)), dma((DEPTH * 4,)),
            dma((2 * steps,)), dma((2 * steps,)),
            dma((4 * nl,)), dma((4 * nl,)),
            dma((2 * nl,)), dma((2 * nl,)),
            dma((8,)), dma((8,)),
        ],
        compiler_params=pltpu.CompilerParams(collective_id=0, has_side_effects=True,
                                             vmem_limit_bytes=48 * 1024 * 1024),
        name='head',
    )(hbm(hidden), hbm(gain.reshape(grows, LANES)), hbm(table.T), hbm(targets), temperature.reshape(1))


def solution(mesh):
    def local_scores(hidden, final_gain, table_cols, targets, temperature):
        probs, ln, tl = _scores(hidden, final_gain, table_cols, targets, temperature)
        return ln.reshape(-1), tl.reshape(-1), probs

    return jax.shard_map(local_scores, mesh=mesh,
                         in_specs=(P('dp', None), P(None), P(None, 'tp'), P('dp'), P()),
                         out_specs=(P('dp'), P('dp'), P('dp', 'tp')),
                         check_vma=False)
```

time: 63 us -> 55.7 us (0.88)
  Pallas kernels: 56.2 us -> 52.5 us
  other arithmetic: 2.5 us -> 0 us
  local copies, waits for them, and re-layouts: 2.76 us -> 1.85 us
    pallas_call x1, Pallas kernels: 56.2 us -> 52.5 us  [_scores(): pl.pallas_call(lambda *refs: _kernel((rows_per, tokens, width, tiles, chu...]
    convert_element_type x1 -> x0, other arithmetic: 2.5 us -> none  [local_scores(): token_probs = jnp.exp(part - stats[:, 0:1]).astype(jnp.bfloat16)]
    unnamed x2 -> x3, local copies, waits for them, and re-layouts: 0.01 us -> 1.85 us
    slice x1 -> x0, local copies, waits for them, and re-layouts: 1.47 us -> none  [local_scores(): return (log_norm, stats[:, 1], token_probs)]
    reshape x1 -> x0, local copies, waits for them, and re-layouts: 1.29 us -> none  [_scores(): gain.reshape(1, -1)]
where the time goes in v2:
time: 55.7 us; the launch traced here: 55.6 us
  Pallas kernels  52.5 us (94%)
  local copies, waits for them, and re-layouts  1.85 us (3%)
  between operations  1.29 us (2%)
    pallas_call x1, Pallas kernels, _scores(): pl.pallas_call(lambda *refs: _kernel((rows_per, tokens, width, tiles, chu...  52.5 us
    unnamed x3, local copies, waits for them, and re-layouts  1.85 us

profile of v2, /device:TPU:0, one launch (start us, length us, event | category | flops | bytes accessed | tf_op | source)
XLA Modules:
  0.0 55.6 jit_solution(18430519287806046753)
XLA Ops:
  1.3 52.5 %head.1 = (bf16[16,18992]{1,0:T(8,128)(2,1)S(1)}, f32[1,16]{1,0:T(1,128)S(1)}, f32[1,16]{1,0:T(1,128)S(1)}) custom-call(bf16[16,1536]{1,0:T(8,128)(2,1)} %refs_0_.1, bf16[12,128]{1,0:T(8,128)(2,1)} %bitcast.9, bf16[192,151936]{1,0:T(8,128)(2,1)} %bitcast.8, s32[16]{0:T(128)} %refs_3_.1, f32[1]{0:T(128)} %bitcast.5.refs_4_), custom_call_target="tpu_custom_call" | custom-call | tf_op jit(solution)/shard_map/head/pallas_call | solution.py:296
  53.8 0.5 copy.11
  54.3 0.5 copy.12
  54.8 0.8 %copy.13 = bf16[16,18992]{1,0:T(8,128)(2,1)} copy(bf16[16,18992]{1,0:T(8,128)(2,1)S(1)} %get-tuple-element.11) | data formatting | bytes 1215488

commit v3 on v2

v3 whole, which is shorter than its diff:
```python
import jax
import jax.numpy as jnp
from jax import lax
from jax.experimental import pallas as pl
from jax.experimental.pallas import tpu as pltpu
from jax.sharding import PartitionSpec as P

NORM_EPS = 1e-6
LANES = 128
LANE_CHUNKS = 5
DEPTH = 4
HEAD = 5 * LANES
NEG = -3.0e38
MESH = pl.DeviceIdType.MESH


def _kernel(shape, hid_hbm, gain_hbm, table_hbm, tgt_hbm, temp, shifted, blocks_ref,
            hid, gain, gain32, tgt, normed, tbuf, psend, prec, own, r1, r2, logits, mine, every,
            in_sem, tsem, head_sem, d2d_rsem, s1_rsem, s2_rsem, st_rsem, out_sem):
    rows_per, tokens, width, tiles, chunk = shape
    half_tiles = tiles // 2
    nl = LANE_CHUNKS
    steps = 4 * nl
    me = lax.axis_index('tp')
    core, mx, my = me % 2, (me // 2) % 2, me // 4
    partner = me + 1 - 2 * core
    xn = me + 2 - 4 * mx
    yn = me + 4 - 8 * my
    first = (xn, yn)
    second = (yn, xn)

    def region_tile(d):
        return (d * rows_per) // LANES - d // 7

    def table_copy(i, q, cut=None):
        p, j = i // nl, i % nl
        lane = q % 2
        a, b = 1 - p // 2, 1 - p % 2
        fx, fy = (a, b) if lane == 0 else (b, a)
        k = 1 - core if q < 2 else core
        d = (my + fy * (1 - 2 * my)) * 4 + (mx + fx * (1 - 2 * mx)) * 2 + k
        tile = region_tile(d) + lane * half_tiles + j * (chunk // LANES)
        col = pl.multiple_of(tile * LANES, LANES)
        slot = (i % DEPTH) * 4 + q
        if cut is None:
            return pltpu.make_async_copy(table_hbm.at[:, pl.ds(col, chunk)], tbuf.at[slot],
                                         tsem.at[slot // 2])
        lo, hi, sem = cut
        return pltpu.make_async_copy(table_hbm.at[:, pl.ds(col + lo, hi - lo)],
                                     tbuf.at[slot, :, pl.ds(lo, hi - lo)], sem)

    small = [pltpu.make_async_copy(src, dst, in_sem.at[n]) for n, (src, dst) in enumerate(
        ((hid_hbm, hid), (gain_hbm, gain), (tgt_hbm, tgt)))]
    small[1].start()
    small[0].start()
    for q in range(2):
        table_copy(0, q, (0, HEAD, head_sem.at[q])).start()
    for q in range(2):
        table_copy(0, q, (HEAD, chunk, tsem.at[0])).start()
    for q in range(2, 4):
        table_copy(0, q).start()

    barrier = pltpu.get_barrier_semaphore()
    for peer in (partner, xn, yn):
        pl.semaphore_signal(barrier, inc=1, device_id={'tp': peer}, device_id_type=MESH)

    small[0].wait()
    h = hid[...].astype(jnp.float32)
    inv_rms = lax.rsqrt(jnp.mean(h * h, axis=-1, keepdims=True) + NORM_EPS)
    small[1].wait()
    gain32[...] = gain[...].astype(jnp.float32)
    g0 = (me * 3) // 2
    hc = hid[:, pl.ds(pl.multiple_of(g0 * LANES, LANES), 2 * LANES)].astype(jnp.float32)
    u0 = hc[:, :LANES] * inv_rms * gain32[pl.ds(g0, 1), :]
    u1 = hc[:, LANES:] * inv_rms * gain32[pl.ds(g0 + 1, 1), :]
    u = jnp.concatenate([u0, u1], axis=1)
    u = jnp.where(core == 0, u[:, :width], u[:, 2 * LANES - width:])
    normed[...] = u.astype(jnp.bfloat16)

    for i in range(1, DEPTH):
        for q in range(4):
            table_copy(i, q).start()
    small[2].start()

    pl.semaphore_wait(barrier, 3)

    def remote(src, dst, kind, recv, device):
        return pltpu.make_async_remote_copy(src_ref=src, dst_ref=dst, send_sem=out_sem.at[kind], recv_sem=recv,
                                            device_id={'tp': device}, device_id_type=MESH)

    def d2d(i, lane):
        return remote(psend.at[i, lane], prec.at[i, lane], 0, d2d_rsem.at[i], partner)

    def d2d_part(lane, lo, hi, sem):
        at = pl.ds(lo, hi - lo)
        return remote(psend.at[0, lane, :, at], prec.at[0, lane, :, at], 0, sem, partner)

    def stage1(lane, i):
        return remote(own.at[i, lane], r1.at[i, lane], 1, s1_rsem.at[i], first[lane])

    def stage1_part(lane, lo, hi):
        at = pl.ds(lo, hi - lo)
        return remote(own.at[0, lane, :, at], r1.at[0, lane, :, at], 1, s1_rsem.at[0], first[lane])

    def stage2(lane, j):
        return remote(own.at[2 * nl + j, lane], r2.at[j, lane], 2, s2_rsem.at[j], second[lane])

    def d2d_pair(i):
        return remote(psend.at[i], prec.at[i], 0, d2d_rsem.at[i], partner)

    def stage1_pair(i):
        return remote(own.at[i], r1.at[i], 1, s1_rsem.at[i], xn)

    def stage2_pair(j):
        return remote(own.at[2 * nl + j], r2.at[j], 2, s2_rsem.at[j], yn)

    def multiply(i, q, cols=slice(None)):
        out = psend if q < 2 else own
        slot = (i % DEPTH) * 4 + q
        out[i, q % 2, :, cols] = jnp.dot(normed[...], tbuf[slot, :, cols], preferred_element_type=jnp.float32)

    def pair_wait(i, half):
        slot = (i % DEPTH) * 4 + half * 2
        both = tbuf.at[pl.ds(slot, 2)]
        pltpu.make_async_copy(both, both, tsem.at[slot // 2]).wait()

    def compute(i, qs, prefetch):
        pair_wait(i, qs[0] // 2)
        for q in qs:
            multiply(i, q)
            if q < 2:
                d2d(i, q).start()
            if prefetch is None:
                @pl.when(i + DEPTH < steps)
                def _():
                    table_copy(i + DEPTH, q).start()
            elif prefetch:
                table_copy(i + DEPTH, q).start()

    theirs, ours = (0, 1), (2, 3)

    def gather_pair(i, send):
        d2d_pair(i).wait_recv()
        for lane in range(2):
            own[i, lane] = own[i, lane] + prec[i, lane]
            if send:
                stage1(lane, i).start()

    for q in range(2):
        table_copy(0, q, (0, HEAD, head_sem.at[q])).wait()
        multiply(0, q, slice(0, HEAD))
        d2d_part(q, 0, HEAD, head_sem.at[2 + q]).start()
    rest = tbuf.at[pl.ds(0, 2), :, pl.ds(HEAD, chunk - HEAD)]
    pltpu.make_async_copy(rest, rest, tsem.at[0]).wait()
    for q in range(2):
        multiply(0, q, slice(HEAD, chunk))
        d2d_part(q, HEAD, chunk, d2d_rsem.at[0]).start()
        table_copy(DEPTH, q).start()
    compute(0, ours, True)
    for lane in range(2):
        d2d_part(lane, 0, HEAD, head_sem.at[2 + lane]).wait_recv()
        own[0, lane, :, :HEAD] = own[0, lane, :, :HEAD] + prec[0, lane, :, :HEAD]
        stage1_part(lane, 0, HEAD).start()
    compute(1, theirs, True)
    tail = pl.ds(HEAD, chunk - HEAD)
    remote(psend.at[0, :, :, tail], prec.at[0, :, :, tail], 0, d2d_rsem.at[0], partner).wait_recv()
    for lane in range(2):
        own[0, lane, :, HEAD:] = own[0, lane, :, HEAD:] + prec[0, lane, :, HEAD:]
        stage1_part(lane, HEAD, chunk).start()
    compute(1, ours, True)
    compute(2, theirs, True)

    def loop_send(i, carry):
        gather_pair(i, True)
        compute(i + 1, ours, True)
        compute(i + 2, theirs, True)
        return carry

    def loop_keep(i, carry):
        gather_pair(i, False)
        compute(i + 1, ours, None)
        compute(i + 2, theirs, None)
        return carry

    lax.fori_loop(1, 2 * nl, loop_send, 0)
    lax.fori_loop(2 * nl, steps - 2, loop_keep, 0)
    gather_pair(steps - 2, False)
    compute(steps - 1, ours, False)
    gather_pair(steps - 1, False)

    def forward(j, carry):
        stage1_pair(j).wait_recv()
        for lane in range(2):
            own[2 * nl + j, lane] = own[2 * nl + j, lane] + r1[j, lane]
            stage2(lane, j).start()
        return carry

    lax.fori_loop(0, nl, forward, 0)

    small[2].wait()
    temperature = temp[0]
    row = lax.broadcasted_iota(jnp.int32, (tokens, LANES), 0)
    lane_id = lax.broadcasted_iota(jnp.int32, (tokens, LANES), 1)
    target = jnp.zeros((tokens, LANES), jnp.int32)
    for t in range(tokens):
        target = jnp.where(row == t, tgt[t], target)
    lo = me * rows_per
    base = region_tile(me) * LANES

    def finish(j, carry):
        m, total, picked = carry
        stage1_pair(nl + j).wait_recv()
        stage2_pair(j).wait_recv()
        for lane in range(2):
            z = own[3 * nl + j, lane] + r1[nl + j, lane] + r2[j, lane]
            t = z / temperature
            off = pl.multiple_of((lane * half_tiles + j * (chunk // LANES)) * LANES, LANES)
            logits[:, pl.ds(off, chunk)] = t
            parts = []
            top = m
            for k in range(chunk // LANES):
                piece = t[:, k * LANES:(k + 1) * LANES]
                col = lane_id + (base + off + k * LANES)
                inside = (col >= lo) & (col < lo + rows_per)
                piece_in = jnp.where(inside, piece, NEG)
                picked = picked + jnp.where(inside & (col == target), piece, 0.0)
                parts.append(piece_in)
                top = jnp.maximum(top, piece_in)
            total = total * jnp.exp(m - top)
            for piece_in in parts:
                total = total + jnp.exp(piece_in - top)
            m = top
        return m, total, picked

    m, total, picked = lax.fori_loop(
        0, nl, finish,
        (jnp.full((tokens, LANES), NEG, jnp.float32), jnp.zeros((tokens, LANES), jnp.float32),
         jnp.zeros((tokens, LANES), jnp.float32)))
    m_row = jnp.max(m, axis=-1, keepdims=True)
    s_row = jnp.sum(total * jnp.exp(m - m_row), axis=-1, keepdims=True)
    p_row = jnp.sum(picked, axis=-1, keepdims=True)
    hs = tokens // 2
    lane8 = lax.broadcasted_iota(jnp.int32, (hs, LANES), 1)
    packed = jnp.broadcast_to(p_row[hs:], (hs, LANES))
    for n, v in enumerate((m_row[:hs], m_row[hs:], s_row[:hs], s_row[hs:], p_row[:hs])):
        packed = jnp.where(lane8 == n, v, packed)
    mine[...] = packed

    def share(peer):
        return remote(mine, every.at[me], 3, st_rsem.at[0], peer)

    far = me + 6 - 4 * mx - 8 * my
    peers = [far, far + 1 - 2 * core, yn, yn + 1 - 2 * core, xn, xn + 1 - 2 * core, partner]
    every[me] = packed
    for peer in peers:
        share(peer).start()

    shift = lo - base
    skip, turn = shift // LANES, shift % LANES
    rot = (LANES - turn) % LANES
    out_tiles = -(-rows_per // LANES)
    keep = lane_id < LANES - turn

    def turned(k):
        at = pl.multiple_of((skip + k) * LANES, LANES)
        return pltpu.roll(logits[:, pl.ds(at, LANES)], rot, axis=1)

    cur = turned(0)
    for k in range(out_tiles):
        if k + 1 < out_tiles:
            nxt = turned(k + 1)
        else:
            nxt = pltpu.roll(logits[:, (tiles - 1) * LANES:tiles * LANES], rot, axis=1)
        shifted[:, k * LANES:(k + 1) * LANES] = jnp.where(keep, cur, nxt)
        cur = nxt

    remote(psend, prec, 0, d2d_rsem.at[0], partner).wait_send()
    sent1 = own.at[pl.ds(0, 2 * nl)]
    remote(sent1, r1, 1, s1_rsem.at[0], xn).wait_send()
    sent2 = own.at[pl.ds(2 * nl, nl)]
    remote(sent2, r2, 2, s2_rsem.at[0], yn).wait_send()

    seven = every.at[pl.ds(0, 7)]
    remote(seven, seven, 3, st_rsem.at[0], partner).wait_recv()
    blocks_ref[...] = every[...]
    remote(seven, seven, 3, st_rsem.at[0], partner).wait_send()


def _finish_kernel(tokens, rows_per, shifted, blocks_ref, probs_hbm, ln_hbm, tl_hbm, probs, ln, tl, sem):
    row = lax.broadcasted_iota(jnp.int32, (tokens, LANES), 0)
    lane_id = lax.broadcasted_iota(jnp.int32, (tokens, LANES), 1)
    blocks = [blocks_ref[d] for d in range(8)]

    def rows16(n):
        return [jnp.concatenate([b[:, n:n + 1], b[:, n + 1:n + 2]], axis=0) for b in blocks]

    ms, ss, ps = rows16(0), rows16(2), rows16(4)
    m_all = ms[0]
    for v in ms[1:]:
        m_all = jnp.maximum(m_all, v)
    s_all = jnp.zeros_like(m_all)
    p_all = jnp.zeros_like(m_all)
    for mv, sv, pv in zip(ms, ss, ps):
        s_all = s_all + sv * jnp.exp(mv - m_all)
        p_all = p_all + pv
    log_norm = m_all + jnp.log(s_all)

    def as_row(v):
        spread = jnp.where(lane_id == row, jnp.broadcast_to(v, (tokens, LANES)), 0.0)
        return jnp.sum(spread, axis=0, keepdims=True)[:, :tokens]
    ln[...] = as_row(log_norm)
    tl[...] = as_row(p_all - log_norm)
    copies = [pltpu.make_async_copy(ln, ln_hbm, sem.at[0]), pltpu.make_async_copy(tl, tl_hbm, sem.at[1])]
    for c in copies:
        c.start()

    step = 19 * LANES
    for at in range(0, rows_per, step):
        end = min(at + step, rows_per)
        probs[:, at:end] = jnp.exp(shifted[:, at:end] - log_norm).astype(jnp.bfloat16)
    copies.append(pltpu.make_async_copy(probs, probs_hbm, sem.at[2]))
    copies[-1].start()
    for c in copies:
        c.wait()


def _scores(hidden, gain, table, targets, temperature):
    tokens, hidden_dim = hidden.shape
    vocab, width = table.shape
    rows_per = vocab // 8
    nl = LANE_CHUNKS
    unit = 2 * nl
    need = -(-rows_per // LANES) + 1
    tiles = -(-need // unit) * unit
    chunk = tiles // unit * LANES
    steps = 4 * nl
    out_tiles = -(-rows_per // LANES)
    f32 = jnp.float32
    dma = pltpu.SemaphoreType.DMA
    block = (tokens, chunk)
    grows = hidden_dim // LANES
    hbm = lambda v: pltpu.with_memory_space_constraint(v, pltpu.HBM)
    shifted, blocks = pl.pallas_call(
        lambda *refs: _kernel((rows_per, tokens, width, tiles, chunk), *refs),
        out_shape=(pltpu.VMEM((tokens, out_tiles * LANES), f32), pltpu.VMEM((8, tokens // 2, LANES), f32)),
        in_specs=[pl.BlockSpec(memory_space=pltpu.HBM)] * 4 + [pl.BlockSpec(memory_space=pltpu.SMEM)],
        out_specs=(pl.BlockSpec(memory_space=pltpu.VMEM),) * 2,
        scratch_shapes=[
            pltpu.VMEM((tokens, hidden_dim), jnp.bfloat16),
            pltpu.VMEM((grows, LANES), jnp.bfloat16),
            pltpu.VMEM((grows, LANES), f32),
            pltpu.SMEM((tokens,), jnp.int32),
            pltpu.VMEM((tokens, width), jnp.bfloat16),
            pltpu.VMEM((DEPTH * 4, width, chunk), jnp.bfloat16),
            pltpu.VMEM((steps, 2) + block, f32),
            pltpu.VMEM((steps, 2) + block, f32),
            pltpu.VMEM((steps, 2) + block, f32),
            pltpu.VMEM((2 * nl, 2) + block, f32),
            pltpu.VMEM((nl, 2) + block, f32),
            pltpu.VMEM((tokens, tiles * LANES), f32),
            pltpu.VMEM((tokens // 2, LANES), f32),
            pltpu.VMEM((8, tokens // 2, LANES), f32),
            dma((3,)), dma((DEPTH * 2,)), dma((4,)),
            dma((steps,)), dma((2 * nl,)), dma((nl,)), dma((1,)), dma((4,)),
        ],
        compiler_params=pltpu.CompilerParams(collective_id=0, has_side_effects=True,
                                             vmem_limit_bytes=48 * 1024 * 1024),
        name='head',
    )(hbm(hidden), hbm(gain.reshape(grows, LANES)), hbm(table.T), hbm(targets), temperature.reshape(1))
    return pl.pallas_call(
        lambda *refs: _finish_kernel(tokens, rows_per, *refs),
        out_shape=(jax.ShapeDtypeStruct((tokens, rows_per), jnp.bfloat16),
                   jax.ShapeDtypeStruct((1, tokens), f32), jax.ShapeDtypeStruct((1, tokens), f32)),
        in_specs=[pl.BlockSpec(memory_space=pltpu.VMEM)] * 2,
        out_specs=(pl.BlockSpec(memory_space=pltpu.HBM),) * 3,
        scratch_shapes=[pltpu.VMEM((tokens, rows_per), jnp.bfloat16), pltpu.VMEM((1, tokens), f32),
                        pltpu.VMEM((1, tokens), f32), dma((3,))],
        compiler_params=pltpu.CompilerParams(vmem_limit_bytes=16 * 1024 * 1024),
        name='finish',
    )(shifted, blocks)


def solution(mesh):
    def local_scores(hidden, final_gain, table_cols, targets, temperature):
        probs, ln, tl = _scores(hidden, final_gain, table_cols, targets, temperature)
        return ln.reshape(-1), tl.reshape(-1), probs

    return jax.shard_map(local_scores, mesh=mesh,
                         in_specs=(P('dp', None), P(None), P(None, 'tp'), P('dp'), P()),
                         out_specs=(P('dp'), P('dp'), P('dp', 'tp')),
                         check_vma=False)
```

time: 55.7 us -> 53.5 us (0.961)
  local copies, waits for them, and re-layouts: 1.85 us -> 0 us
    unnamed x3 -> x0, local copies, waits for them, and re-layouts: 1.85 us -> none
    pallas_call x1, Pallas kernels: 52.5 us -> 50.8 us  [_scores(): pl.pallas_call(lambda *refs: _kernel((rows_per, tokens, width, tiles, chu...]
    pallas_call x0 -> x1, Pallas kernels: none -> 1.26 us  [_scores(): pl.pallas_call(lambda *refs: _finish_kernel(tokens, rows_per, *refs), out...]
where the time goes in v3:
time: 53.5 us; the launch traced here: 53.3 us
  Pallas kernels  52.1 us (97%)
  between operations  1.29 us (2%)
    pallas_call x1, Pallas kernels, _scores(): pl.pallas_call(lambda *refs: _kernel((rows_per, tokens, width, tiles, chu...  50.8 us
    pallas_call x1, Pallas kernels, _scores(): pl.pallas_call(lambda *refs: _finish_kernel(tokens, rows_per, *refs), out...  1.26 us

profile of v3, /device:TPU:0, one launch (start us, length us, event | category | flops | bytes accessed | tf_op | source)
XLA Modules:
  0.0 53.3 jit_solution(11052773222461894263)
XLA Ops:
  1.3 50.8 %head.1 = (f32[16,19072]{1,0:T(8,128)S(1)}, f32[8,8,128]{2,1,0:T(8,128)S(1)}) custom-call(bf16[16,1536]{1,0:T(8,128)(2,1)} %refs_0_.1, bf16[12,128]{1,0:T(8,128)(2,1)} %bitcast.7, bf16[192,151936]{1,0:T(8,128)(2,1)} %bitcast.6, s32[16]{0:T(128)} %refs_3_.1, f32[1]{0:T(128)} %bitcast.5.refs_4_), custom_call_target="tpu_custom_call" | custom-call | tf_op jit(solution)/shard_map/head/pallas_call | solution.py:343
  52.1 1.3 %finish.1 = (bf16[16,18992]{1,0:T(8,128)(2,1)}, f32[1,16]{1,0:T(1,128)}, f32[1,16]{1,0:T(1,128)}) custom-call(f32[16,19072]{1,0:T(8,128)S(1)} %get-tuple-element.8.refs_0_, f32[8,8,128]{2,1,0:T(8,128)S(1)} %get-tuple-element.9.refs_1_), custom_call_target="tpu_custom_call" | custom-call | tf_op jit(solution)/shard_map/finish/pallas_call | solution.py:370

commit v4 on v3

--- a/solution.py
+++ b/solution.py
@@ -51,20 +51,18 @@
 
     small = [pltpu.make_async_copy(src, dst, in_sem.at[n]) for n, (src, dst) in enumerate(
         ((hid_hbm, hid), (gain_hbm, gain), (tgt_hbm, tgt)))]
+    small[0].start()
     small[1].start()
-    small[0].start()
-    for q in range(2):
-        table_copy(0, q, (0, HEAD, head_sem.at[q])).start()
-    for q in range(2):
-        table_copy(0, q, (HEAD, chunk, tsem.at[0])).start()
-    for q in range(2, 4):
-        table_copy(0, q).start()
+    for q in range(4):
+        table_copy(0, q, (0, HEAD, head_sem.at[min(q, 2)])).start()
 
     barrier = pltpu.get_barrier_semaphore()
     for peer in (partner, xn, yn):
         pl.semaphore_signal(barrier, inc=1, device_id={'tp': peer}, device_id_type=MESH)
 
     small[0].wait()
+    for q in range(4):
+        table_copy(0, q, (HEAD, chunk, tsem.at[q // 2])).start()
     h = hid[...].astype(jnp.float32)
     inv_rms = lax.rsqrt(jnp.mean(h * h, axis=-1, keepdims=True) + NORM_EPS)
     small[1].wait()
@@ -77,11 +75,6 @@
     u = jnp.where(core == 0, u[:, :width], u[:, 2 * LANES - width:])
     normed[...] = u.astype(jnp.bfloat16)
 
-    for i in range(1, DEPTH):
-        for q in range(4):
-            table_copy(i, q).start()
-    small[2].start()
-
     pl.semaphore_wait(barrier, 3)
 
     def remote(src, dst, kind, recv, device):
@@ -89,14 +82,14 @@
                                             device_id={'tp': device}, device_id_type=MESH)
 
     def d2d(i, lane):
-        return remote(psend.at[i, lane], prec.at[i, lane], 0, d2d_rsem.at[i], partner)
+        return remote(psend.at[i, lane], prec.at[i, lane], 0, d2d_rsem.at[i - (i // (2 * nl)) * (i - 2 * nl)], partner)
 
     def d2d_part(lane, lo, hi, sem):
         at = pl.ds(lo, hi - lo)
         return remote(psend.at[0, lane, :, at], prec.at[0, lane, :, at], 0, sem, partner)
 
     def stage1(lane, i):
-        return remote(own.at[i, lane], r1.at[i, lane], 1, s1_rsem.at[i], first[lane])
+        return remote(own.at[i, lane], r1.at[i, lane], 1, s1_rsem.at[i // nl], first[lane])
 
     def stage1_part(lane, lo, hi):
         at = pl.ds(lo, hi - lo)
@@ -107,9 +100,6 @@
 
     def d2d_pair(i):
         return remote(psend.at[i], prec.at[i], 0, d2d_rsem.at[i], partner)
-
-    def stage1_pair(i):
-        return remote(own.at[i], r1.at[i], 1, s1_rsem.at[i], xn)
 
     def stage2_pair(j):
         return remote(own.at[2 * nl + j], r2.at[j], 2, s2_rsem.at[j], yn)
@@ -139,28 +129,33 @@
 
     theirs, ours = (0, 1), (2, 3)
 
-    def gather_pair(i, send):
-        d2d_pair(i).wait_recv()
-        for lane in range(2):
-            own[i, lane] = own[i, lane] + prec[i, lane]
-            if send:
-                stage1(lane, i).start()
+    def piece(half, lo, hi):
+        return tbuf.at[pl.ds(2 * half, 2), :, pl.ds(lo, hi - lo)]
 
     for q in range(2):
         table_copy(0, q, (0, HEAD, head_sem.at[q])).wait()
         multiply(0, q, slice(0, HEAD))
-        d2d_part(q, 0, HEAD, head_sem.at[2 + q]).start()
-    rest = tbuf.at[pl.ds(0, 2), :, pl.ds(HEAD, chunk - HEAD)]
-    pltpu.make_async_copy(rest, rest, tsem.at[0]).wait()
+        d2d_part(q, 0, HEAD, head_sem.at[3 + q]).start()
+    pltpu.make_async_copy(piece(1, 0, HEAD), piece(1, 0, HEAD), head_sem.at[2]).wait()
+    for q in range(2, 4):
+        multiply(0, q, slice(0, HEAD))
+    for i in range(1, DEPTH):
+        for q in range(4):
+            table_copy(i, q).start()
+    small[2].start()
+    pltpu.make_async_copy(piece(0, HEAD, chunk), piece(0, HEAD, chunk), tsem.at[0]).wait()
     for q in range(2):
         multiply(0, q, slice(HEAD, chunk))
         d2d_part(q, HEAD, chunk, d2d_rsem.at[0]).start()
         table_copy(DEPTH, q).start()
-    compute(0, ours, True)
     for lane in range(2):
-        d2d_part(lane, 0, HEAD, head_sem.at[2 + lane]).wait_recv()
+        d2d_part(lane, 0, HEAD, head_sem.at[3 + lane]).wait_recv()
         own[0, lane, :, :HEAD] = own[0, lane, :, :HEAD] + prec[0, lane, :, :HEAD]
         stage1_part(lane, 0, HEAD).start()
+    pltpu.make_async_copy(piece(1, HEAD, chunk), piece(1, HEAD, chunk), tsem.at[1]).wait()
+    for q in range(2, 4):
+        multiply(0, q, slice(HEAD, chunk))
+        table_copy(DEPTH, q).start()
     compute(1, theirs, True)
     tail = pl.ds(HEAD, chunk - HEAD)
     remote(psend.at[0, :, :, tail], prec.at[0, :, :, tail], 0, d2d_rsem.at[0], partner).wait_recv()
@@ -171,31 +166,37 @@
     compute(2, theirs, True)
 
     def loop_send(i, carry):
-        gather_pair(i, True)
+        d2d_pair(i).wait_recv()
+        for lane in range(2):
+            own[i, lane] = own[i, lane] + prec[i, lane]
+            stage1(lane, i).start()
         compute(i + 1, ours, True)
         compute(i + 2, theirs, True)
         return carry
 
     def loop_keep(i, carry):
-        gather_pair(i, False)
-        compute(i + 1, ours, None)
-        compute(i + 2, theirs, None)
+        compute(i, ours, None)
+        compute(i + 1, theirs, None)
         return carry
 
     lax.fori_loop(1, 2 * nl, loop_send, 0)
-    lax.fori_loop(2 * nl, steps - 2, loop_keep, 0)
-    gather_pair(steps - 2, False)
+    lax.fori_loop(2 * nl + 1, steps - 1, loop_keep, 0)
     compute(steps - 1, ours, False)
-    gather_pair(steps - 1, False)
+
+    late = pl.ds(2 * nl, 2 * nl)
+    remote(psend.at[late], prec.at[late], 0, d2d_rsem.at[2 * nl], partner).wait_recv()
+    relay, near = pl.ds(0, nl), pl.ds(nl, nl)
+    remote(own.at[relay], r1.at[relay], 1, s1_rsem.at[0], xn).wait_recv()
 
     def forward(j, carry):
-        stage1_pair(j).wait_recv()
+        i = 2 * nl + j
         for lane in range(2):
-            own[2 * nl + j, lane] = own[2 * nl + j, lane] + r1[j, lane]
+            own[i, lane] = own[i, lane] + prec[i, lane] + r1[j, lane]
             stage2(lane, j).start()
         return carry
 
     lax.fori_loop(0, nl, forward, 0)
+    remote(own.at[near], r1.at[near], 1, s1_rsem.at[1], xn).wait_recv()
 
     small[2].wait()
     temperature = temp[0]
@@ -209,10 +210,10 @@
 
     def finish(j, carry):
         m, total, picked = carry
-        stage1_pair(nl + j).wait_recv()
+        mine_at = 3 * nl + j
         stage2_pair(j).wait_recv()
         for lane in range(2):
-            z = own[3 * nl + j, lane] + r1[nl + j, lane] + r2[j, lane]
+            z = own[mine_at, lane] + prec[mine_at, lane] + r1[nl + j, lane] + r2[j, lane]
             t = z / temperature
             off = pl.multiple_of((lane * half_tiles + j * (chunk // LANES)) * LANES, LANES)
             logits[:, pl.ds(off, chunk)] = t
@@ -271,7 +272,7 @@
             nxt = turned(k + 1)
         else:
             nxt = pltpu.roll(logits[:, (tiles - 1) * LANES:tiles * LANES], rot, axis=1)
-        shifted[:, k * LANES:(k + 1) * LANES] = jnp.where(keep, cur, nxt)
+        shifted[:, k * LANES:(k + 1) * LANES] = jnp.exp(jnp.where(keep, cur, nxt) - m_row)
         cur = nxt
 
     remote(psend, prec, 0, d2d_rsem.at[0], partner).wait_send()
@@ -290,6 +291,7 @@
     row = lax.broadcasted_iota(jnp.int32, (tokens, LANES), 0)
     lane_id = lax.broadcasted_iota(jnp.int32, (tokens, LANES), 1)
     blocks = [blocks_ref[d] for d in range(8)]
+    mb = blocks_ref[lax.axis_index('tp')]
 
     def rows16(n):
         return [jnp.concatenate([b[:, n:n + 1], b[:, n + 1:n + 2]], axis=0) for b in blocks]
@@ -314,12 +316,17 @@
     for c in copies:
         c.start()
 
+    scale = jnp.exp(jnp.concatenate([mb[:, 0:1], mb[:, 1:2]], axis=0) - log_norm)
     step = 19 * LANES
+    cut = 4 * step
     for at in range(0, rows_per, step):
         end = min(at + step, rows_per)
-        probs[:, at:end] = jnp.exp(shifted[:, at:end] - log_norm).astype(jnp.bfloat16)
-    copies.append(pltpu.make_async_copy(probs, probs_hbm, sem.at[2]))
-    copies[-1].start()
+        probs[:, at:end] = (shifted[:, at:end] * scale).astype(jnp.bfloat16)
+        if end == cut or end == rows_per:
+            side = pl.ds(0, cut) if end == cut else pl.ds(cut, rows_per - cut)
+            n = 2 if end == cut else 3
+            copies.append(pltpu.make_async_copy(probs.at[:, side], probs_hbm.at[:, side], sem.at[n]))
+            copies[-1].start()
     for c in copies:
         c.wait()
 
@@ -360,8 +367,8 @@
             pltpu.VMEM((tokens, tiles * LANES), f32),
             pltpu.VMEM((tokens // 2, LANES), f32),
             pltpu.VMEM((8, tokens // 2, LANES), f32),
-            dma((3,)), dma((DEPTH * 2,)), dma((4,)),
-            dma((steps,)), dma((2 * nl,)), dma((nl,)), dma((1,)), dma((4,)),
+            dma((3,)), dma((DEPTH * 2,)), dma((5,)),
+            dma((2 * nl + 1,)), dma((2,)), dma((nl,)), dma((1,)), dma((4,)),
         ],
         compiler_params=pltpu.CompilerParams(collective_id=0, has_side_effects=True,
                                              vmem_limit_bytes=48 * 1024 * 1024),
@@ -374,7 +381,7 @@
         in_specs=[pl.BlockSpec(memory_space=pltpu.VMEM)] * 2,
         out_specs=(pl.BlockSpec(memory_space=pltpu.HBM),) * 3,
         scratch_shapes=[pltpu.VMEM((tokens, rows_per), jnp.bfloat16), pltpu.VMEM((1, tokens), f32),
-                        pltpu.VMEM((1, tokens), f32), dma((3,))],
+                        pltpu.VMEM((1, tokens), f32), dma((4,))],
         compiler_params=pltpu.CompilerParams(vmem_limit_bytes=16 * 1024 * 1024),
         name='finish',
     )(shifted, blocks)

time: 53.5 us -> 53.2 us (level)
  no operation moved by 1% of the time
where the time goes in v4:
time: 53.2 us; the launch traced here: 53.1 us
  Pallas kernels  51.8 us (97%)
  between operations  1.29 us (2%)
    pallas_call x1, Pallas kernels, _scores(): pl.pallas_call(lambda *refs: _kernel((rows_per, tokens, width, tiles, chu...  50.5 us
    pallas_call x1, Pallas kernels, _scores(): pl.pallas_call(lambda *refs: _finish_kernel(tokens, rows_per, *refs), out...  1.26 us

profile of v4, /device:TPU:0, one launch (start us, length us, event | category | flops | bytes accessed | tf_op | source)
XLA Modules:
  0.0 53.1 jit_solution(13049139993381444969)
XLA Ops:
  1.3 50.5 %head.1 = (f32[16,19072]{1,0:T(8,128)S(1)}, f32[8,8,128]{2,1,0:T(8,128)S(1)}) custom-call(bf16[16,1536]{1,0:T(8,128)(2,1)} %refs_0_.1, bf16[12,128]{1,0:T(8,128)(2,1)} %bitcast.7, bf16[192,151936]{1,0:T(8,128)(2,1)} %bitcast.6, s32[16]{0:T(128)} %refs_3_.1, f32[1]{0:T(128)} %bitcast.5.refs_4_), custom_call_target="tpu_custom_call" | custom-call | tf_op jit(solution)/shard_map/head/pallas_call | solution.py:350
  51.8 1.3 %finish.1 = (bf16[16,18992]{1,0:T(8,128)(2,1)}, f32[1,16]{1,0:T(1,128)}, f32[1,16]{1,0:T(1,128)}) custom-call(f32[16,19072]{1,0:T(8,128)S(1)} %get-tuple-element.8.refs_0_, f32[8,8,128]{2,1,0:T(8,128)S(1)} %get-tuple-element.9.refs_1_), custom_call_target="tpu_custom_call" | custom-call | tf_op jit(solution)/shard_map/finish/pallas_call | solution.py:377

commit v5 on v4

--- a/solution.py
+++ b/solution.py
@@ -7,9 +7,11 @@
 
 NORM_EPS = 1e-6
 LANES = 128
-LANE_CHUNKS = 5
-DEPTH = 4
-HEAD = 5 * LANES
+LANE_CHUNKS = 3
+DEPTH = 3
+HEAD, MID = 4 * LANES, 11 * LANES
+LAST = 5 * LANES
+GROUP = 5
 NEG = -3.0e38
 MESH = pl.DeviceIdType.MESH
 
@@ -53,16 +55,24 @@
         ((hid_hbm, hid), (gain_hbm, gain), (tgt_hbm, tgt)))]
     small[0].start()
     small[1].start()
-    for q in range(4):
-        table_copy(0, q, (0, HEAD, head_sem.at[min(q, 2)])).start()
+    def first_copy(n):
+        q = n % 4
+        if n < 4:
+            return table_copy(0, q, (0, HEAD, head_sem.at[min(q, 2)]))
+        if n < 8:
+            return table_copy(0, q, (HEAD, MID, head_sem.at[3 + q // 2]))
+        return table_copy(0, q, (MID, chunk, tsem.at[q // 2]))
+
+    for n in (0, 1, 2, 3):
+        first_copy(n).start()
 
     barrier = pltpu.get_barrier_semaphore()
     for peer in (partner, xn, yn):
         pl.semaphore_signal(barrier, inc=1, device_id={'tp': peer}, device_id_type=MESH)
 
     small[0].wait()
-    for q in range(4):
-        table_copy(0, q, (HEAD, chunk, tsem.at[q // 2])).start()
+    for n in (4, 5):
+        first_copy(n).start()
     h = hid[...].astype(jnp.float32)
     inv_rms = lax.rsqrt(jnp.mean(h * h, axis=-1, keepdims=True) + NORM_EPS)
     small[1].wait()
@@ -74,6 +84,8 @@
     u = jnp.concatenate([u0, u1], axis=1)
     u = jnp.where(core == 0, u[:, :width], u[:, 2 * LANES - width:])
     normed[...] = u.astype(jnp.bfloat16)
+    for n in (6, 7, 8, 9, 10, 11):
+        first_copy(n).start()
 
     pl.semaphore_wait(barrier, 3)
 
@@ -95,14 +107,16 @@
         at = pl.ds(lo, hi - lo)
         return remote(own.at[0, lane, :, at], r1.at[0, lane, :, at], 1, s1_rsem.at[0], first[lane])
 
-    def stage2(lane, j):
-        return remote(own.at[2 * nl + j, lane], r2.at[j, lane], 2, s2_rsem.at[j], second[lane])
+    def stage2(lane, j, lo, hi, sem):
+        at = pl.ds(lo, hi - lo)
+        return remote(own.at[2 * nl + j, lane, :, at], r2.at[j, lane, :, at], 2, s2_rsem.at[sem], second[lane])
 
     def d2d_pair(i):
         return remote(psend.at[i], prec.at[i], 0, d2d_rsem.at[i], partner)
 
-    def stage2_pair(j):
-        return remote(own.at[2 * nl + j], r2.at[j], 2, s2_rsem.at[j], yn)
+    def stage2_pair(j, lo, hi, sem):
+        at = pl.ds(lo, hi - lo)
+        return remote(own.at[2 * nl + j, :, :, at], r2.at[j, :, :, at], 2, s2_rsem.at[sem], yn)
 
     def multiply(i, q, cols=slice(None)):
         out = psend if q < 2 else own
@@ -132,36 +146,52 @@
     def piece(half, lo, hi):
         return tbuf.at[pl.ds(2 * half, 2), :, pl.ds(lo, hi - lo)]
 
+    def landed(half, lo, hi, sem):
+        pltpu.make_async_copy(piece(half, lo, hi), piece(half, lo, hi), sem).wait()
+
+    def head_pair(lo, hi, sem):
+        at = pl.ds(lo, hi - lo)
+        remote(psend.at[0, :, :, at], prec.at[0, :, :, at], 0, sem, partner).wait_recv()
+        for lane in range(2):
+            own[0, lane, :, lo:hi] = own[0, lane, :, lo:hi] + prec[0, lane, :, lo:hi]
+            stage1_part(lane, lo, hi).start()
+
     for q in range(2):
-        table_copy(0, q, (0, HEAD, head_sem.at[q])).wait()
+        first_copy(q).wait()
         multiply(0, q, slice(0, HEAD))
-        d2d_part(q, 0, HEAD, head_sem.at[3 + q]).start()
-    pltpu.make_async_copy(piece(1, 0, HEAD), piece(1, 0, HEAD), head_sem.at[2]).wait()
+        d2d_part(q, 0, HEAD, head_sem.at[5 + q]).start()
+    landed(1, 0, HEAD, head_sem.at[2])
     for q in range(2, 4):
         multiply(0, q, slice(0, HEAD))
-    for i in range(1, DEPTH):
+    landed(0, HEAD, MID, head_sem.at[3])
+    for q in range(2):
+        multiply(0, q, slice(HEAD, MID))
+        d2d_part(q, HEAD, MID, head_sem.at[7]).start()
+    for q in range(4):
+        table_copy(1, q).start()
+    for lane in range(2):
+        d2d_part(lane, 0, HEAD, head_sem.at[5 + lane]).wait_recv()
+        own[0, lane, :, :HEAD] = own[0, lane, :, :HEAD] + prec[0, lane, :, :HEAD]
+        stage1_part(lane, 0, HEAD).start()
+    landed(0, MID, chunk, tsem.at[0])
+    for q in range(2):
+        multiply(0, q, slice(MID, chunk))
+        d2d_part(q, MID, chunk, d2d_rsem.at[0]).start()
+    landed(1, HEAD, MID, head_sem.at[4])
+    for q in range(2, 4):
+        multiply(0, q, slice(HEAD, MID))
+    head_pair(HEAD, MID, head_sem.at[7])
+    for i in range(2, DEPTH):
         for q in range(4):
             table_copy(i, q).start()
+    landed(1, MID, chunk, tsem.at[1])
+    for q in range(2, 4):
+        multiply(0, q, slice(MID, chunk))
+    for q in range(4):
+        table_copy(DEPTH, q).start()
     small[2].start()
-    pltpu.make_async_copy(piece(0, HEAD, chunk), piece(0, HEAD, chunk), tsem.at[0]).wait()
-    for q in range(2):
-        multiply(0, q, slice(HEAD, chunk))
-        d2d_part(q, HEAD, chunk, d2d_rsem.at[0]).start()
-        table_copy(DEPTH, q).start()
-    for lane in range(2):
-        d2d_part(lane, 0, HEAD, head_sem.at[3 + lane]).wait_recv()
-        own[0, lane, :, :HEAD] = own[0, lane, :, :HEAD] + prec[0, lane, :, :HEAD]
-        stage1_part(lane, 0, HEAD).start()
-    pltpu.make_async_copy(piece(1, HEAD, chunk), piece(1, HEAD, chunk), tsem.at[1]).wait()
-    for q in range(2, 4):
-        multiply(0, q, slice(HEAD, chunk))
-        table_copy(DEPTH, q).start()
+    head_pair(MID, chunk, d2d_rsem.at[0])
     compute(1, theirs, True)
-    tail = pl.ds(HEAD, chunk - HEAD)
-    remote(psend.at[0, :, :, tail], prec.at[0, :, :, tail], 0, d2d_rsem.at[0], partner).wait_recv()
-    for lane in range(2):
-        own[0, lane, :, HEAD:] = own[0, lane, :, HEAD:] + prec[0, lane, :, HEAD:]
-        stage1_part(lane, HEAD, chunk).start()
     compute(1, ours, True)
     compute(2, theirs, True)
 
@@ -188,75 +218,73 @@
     relay, near = pl.ds(0, nl), pl.ds(nl, nl)
     remote(own.at[relay], r1.at[relay], 1, s1_rsem.at[0], xn).wait_recv()
 
-    def forward(j, carry):
+    pieces = [(j, 0, chunk) for j in range(nl - 1)] + [(nl - 1, 0, chunk - LAST), (nl - 1, chunk - LAST, chunk)]
+
+    for n, (j, lo, hi) in enumerate(pieces):
         i = 2 * nl + j
         for lane in range(2):
-            own[i, lane] = own[i, lane] + prec[i, lane] + r1[j, lane]
-            stage2(lane, j).start()
-        return carry
-
-    lax.fori_loop(0, nl, forward, 0)
+            own[i, lane, :, lo:hi] = own[i, lane, :, lo:hi] + prec[i, lane, :, lo:hi] + r1[j, lane, :, lo:hi]
+            stage2(lane, j, lo, hi, n).start()
+
     remote(own.at[near], r1.at[near], 1, s1_rsem.at[1], xn).wait_recv()
 
     small[2].wait()
-    temperature = temp[0]
+    inv_temp = 1.0 / jnp.full((tokens, LANES), temp[0], jnp.float32)
     row = lax.broadcasted_iota(jnp.int32, (tokens, LANES), 0)
     lane_id = lax.broadcasted_iota(jnp.int32, (tokens, LANES), 1)
     target = jnp.zeros((tokens, LANES), jnp.int32)
     for t in range(tokens):
         target = jnp.where(row == t, tgt[t], target)
-    lo = me * rows_per
-    base = region_tile(me) * LANES
-
-    def finish(j, carry):
-        m, total, picked = carry
-        mine_at = 3 * nl + j
-        stage2_pair(j).wait_recv()
+    lo_row = me * rows_per
+    shift = lo_row - region_tile(me) * LANES
+    rel = target - lo_row
+    rel = jnp.where((rel >= 0) & (rel < rows_per), rel + shift, -1)
+    edge = (0, 1, tiles - 2, tiles - 1)
+
+    m = jnp.full((tokens, LANES), NEG, jnp.float32)
+    total = jnp.zeros((tokens, LANES), jnp.float32)
+    picked = jnp.zeros((tokens, LANES), jnp.float32)
+    for n, (j, lo, hi) in enumerate(pieces):
+        i = 3 * nl + j
+        stage2_pair(j, lo, hi, n).wait_recv()
         for lane in range(2):
-            z = own[mine_at, lane] + prec[mine_at, lane] + r1[nl + j, lane] + r2[j, lane]
-            t = z / temperature
-            off = pl.multiple_of((lane * half_tiles + j * (chunk // LANES)) * LANES, LANES)
-            logits[:, pl.ds(off, chunk)] = t
-            parts = []
-            top = m
-            for k in range(chunk // LANES):
-                piece = t[:, k * LANES:(k + 1) * LANES]
-                col = lane_id + (base + off + k * LANES)
-                inside = (col >= lo) & (col < lo + rows_per)
-                piece_in = jnp.where(inside, piece, NEG)
-                picked = picked + jnp.where(inside & (col == target), piece, 0.0)
-                parts.append(piece_in)
-                top = jnp.maximum(top, piece_in)
-            total = total * jnp.exp(m - top)
-            for piece_in in parts:
-                total = total + jnp.exp(piece_in - top)
-            m = top
-        return m, total, picked
-
-    m, total, picked = lax.fori_loop(
-        0, nl, finish,
-        (jnp.full((tokens, LANES), NEG, jnp.float32), jnp.zeros((tokens, LANES), jnp.float32),
-         jnp.zeros((tokens, LANES), jnp.float32)))
+            for at in range(lo, hi, GROUP * LANES):
+                parts = []
+                top = m
+                for k in range(GROUP):
+                    c = slice(at + k * LANES, at + (k + 1) * LANES)
+                    tile = lane * half_tiles + j * (chunk // LANES) + at // LANES + k
+                    z = own[i, lane, :, c] + prec[i, lane, :, c] + r1[nl + j, lane, :, c] + r2[j, lane, :, c]
+                    t = z * inv_temp
+                    logits[:, tile * LANES:(tile + 1) * LANES] = t
+                    picked = picked + jnp.where(lane_id == rel - tile * LANES, t, 0.0)
+                    if tile in edge:
+                        col = lane_id + (tile * LANES - shift)
+                        t = jnp.where((col >= 0) & (col < rows_per), t, NEG)
+                    parts.append(t)
+                    top = jnp.maximum(top, t)
+                total = total * jnp.exp(m - top)
+                for t in parts:
+                    total = total + jnp.exp(t - top)
+                m = top
     m_row = jnp.max(m, axis=-1, keepdims=True)
     s_row = jnp.sum(total * jnp.exp(m - m_row), axis=-1, keepdims=True)
     p_row = jnp.sum(picked, axis=-1, keepdims=True)
     hs = tokens // 2
     lane8 = lax.broadcasted_iota(jnp.int32, (hs, LANES), 1)
-    packed = jnp.broadcast_to(p_row[hs:], (hs, LANES))
-    for n, v in enumerate((m_row[:hs], m_row[hs:], s_row[:hs], s_row[hs:], p_row[:hs])):
-        packed = jnp.where(lane8 == n, v, packed)
-    mine[...] = packed
+    mine[0] = jnp.where(lane8 < 64, jnp.where(lane8 < 32, m_row[:hs], m_row[hs:]),
+                        jnp.where(lane8 < 96, p_row[:hs], p_row[hs:]))
+    mine[1] = jnp.where(lane8 < 32, s_row[:hs], s_row[hs:])
 
     def share(peer):
         return remote(mine, every.at[me], 3, st_rsem.at[0], peer)
 
     far = me + 6 - 4 * mx - 8 * my
     peers = [far, far + 1 - 2 * core, yn, yn + 1 - 2 * core, xn, xn + 1 - 2 * core, partner]
-    every[me] = packed
+    every[me] = mine[...]
     for peer in peers:
         share(peer).start()
 
-    shift = lo - base
     skip, turn = shift // LANES, shift % LANES
     rot = (LANES - turn) % LANES
     out_tiles = -(-rows_per // LANES)
@@ -290,43 +318,37 @@
 def _finish_kernel(tokens, rows_per, shifted, blocks_ref, probs_hbm, ln_hbm, tl_hbm, probs, ln, tl, sem):
     row = lax.broadcasted_iota(jnp.int32, (tokens, LANES), 0)
     lane_id = lax.broadcasted_iota(jnp.int32, (tokens, LANES), 1)
-    blocks = [blocks_ref[d] for d in range(8)]
-    mb = blocks_ref[lax.axis_index('tp')]
-
-    def rows16(n):
-        return [jnp.concatenate([b[:, n:n + 1], b[:, n + 1:n + 2]], axis=0) for b in blocks]
-
-    ms, ss, ps = rows16(0), rows16(2), rows16(4)
-    m_all = ms[0]
-    for v in ms[1:]:
-        m_all = jnp.maximum(m_all, v)
-    s_all = jnp.zeros_like(m_all)
-    p_all = jnp.zeros_like(m_all)
-    for mv, sv, pv in zip(ms, ss, ps):
-        s_all = s_all + sv * jnp.exp(mv - m_all)
-        p_all = p_all + pv
-    log_norm = m_all + jnp.log(s_all)
+    def tree(op, vs):
+        while len(vs) > 1:
+            vs = [op(vs[k], vs[k + 1]) for k in range(0, len(vs), 2)]
+        return vs[0]
+
+    def rows16(v, at):
+        return jnp.concatenate([v[:, at:at + 1], v[:, at + 32:at + 33]], axis=0)
+
+    tops = [blocks_ref[d, 0] for d in range(8)]
+    m_all = tree(jnp.maximum, tops)
+    s_all = tree(jnp.add, [blocks_ref[d, 1] * jnp.exp(tops[d] - m_all) for d in range(8)])
+    log_all = m_all + jnp.log(s_all)
+    scale = rows16(jnp.exp(blocks_ref[lax.axis_index('tp'), 0] - log_all), 0)
+    log_norm = rows16(log_all, 0)
+    p_all = rows16(tree(jnp.add, tops), 64)
 
     def as_row(v):
         spread = jnp.where(lane_id == row, jnp.broadcast_to(v, (tokens, LANES)), 0.0)
         return jnp.sum(spread, axis=0, keepdims=True)[:, :tokens]
+
+    cut = 76 * LANES
+    sides = (pl.ds(0, cut), pl.ds(cut, rows_per - cut))
+    copies = [pltpu.make_async_copy(probs.at[:, side], probs_hbm.at[:, side], sem.at[n]) for n, side in enumerate(sides)]
+    copies += [pltpu.make_async_copy(ln, ln_hbm, sem.at[2]), pltpu.make_async_copy(tl, tl_hbm, sem.at[3])]
+    probs[:, :cut] = (shifted[:, :cut] * scale).astype(jnp.bfloat16)
+    copies[0].start()
     ln[...] = as_row(log_norm)
     tl[...] = as_row(p_all - log_norm)
-    copies = [pltpu.make_async_copy(ln, ln_hbm, sem.at[0]), pltpu.make_async_copy(tl, tl_hbm, sem.at[1])]
-    for c in copies:
+    probs[:, cut:rows_per] = (shifted[:, cut:rows_per] * scale).astype(jnp.bfloat16)
+    for c in copies[1:]:
         c.start()
-
-    scale = jnp.exp(jnp.concatenate([mb[:, 0:1], mb[:, 1:2]], axis=0) - log_norm)
-    step = 19 * LANES
-    cut = 4 * step
-    for at in range(0, rows_per, step):
-        end = min(at + step, rows_per)
-        probs[:, at:end] = (shifted[:, at:end] * scale).astype(jnp.bfloat16)
-        if end == cut or end == rows_per:
-            side = pl.ds(0, cut) if end == cut else pl.ds(cut, rows_per - cut)
-            n = 2 if end == cut else 3
-            copies.append(pltpu.make_async_copy(probs.at[:, side], probs_hbm.at[:, side], sem.at[n]))
-            copies[-1].start()
     for c in copies:
         c.wait()
 
@@ -349,7 +371,7 @@
     hbm = lambda v: pltpu.with_memory_space_constraint(v, pltpu.HBM)
     shifted, blocks = pl.pallas_call(
         lambda *refs: _kernel((rows_per, tokens, width, tiles, chunk), *refs),
-        out_shape=(pltpu.VMEM((tokens, out_tiles * LANES), f32), pltpu.VMEM((8, tokens // 2, LANES), f32)),
+        out_shape=(pltpu.VMEM((tokens, out_tiles * LANES), f32), pltpu.VMEM((8, 2, tokens // 2, LANES), f32)),
         in_specs=[pl.BlockSpec(memory_space=pltpu.HBM)] * 4 + [pl.BlockSpec(memory_space=pltpu.SMEM)],
         out_specs=(pl.BlockSpec(memory_space=pltpu.VMEM),) * 2,
         scratch_shapes=[
@@ -365,10 +387,10 @@
             pltpu.VMEM((2 * nl, 2) + block, f32),
             pltpu.VMEM((nl, 2) + block, f32),
             pltpu.VMEM((tokens, tiles * LANES), f32),
-            pltpu.VMEM((tokens // 2, LANES), f32),
-            pltpu.VMEM((8, tokens // 2, LANES), f32),
-            dma((3,)), dma((DEPTH * 2,)), dma((5,)),
-            dma((2 * nl + 1,)), dma((2,)), dma((nl,)), dma((1,)), dma((4,)),
+            pltpu.VMEM((2, tokens // 2, LANES), f32),
+            pltpu.VMEM((8, 2, tokens // 2, LANES), f32),
+            dma((3,)), dma((DEPTH * 2,)), dma((8,)),
+            dma((2 * nl + 1,)), dma((2,)), dma((nl + 1,)), dma((1,)), dma((4,)),
         ],
         compiler_params=pltpu.CompilerParams(collective_id=0, has_side_effects=True,
                                              vmem_limit_bytes=48 * 1024 * 1024),

time: 53.2 us -> 52.9 us (level)
  no operation moved by 1% of the time
where the time goes in v5:
time: 52.9 us; the launch traced here: 52.8 us
  Pallas kernels  51.5 us (97%)
  between operations  1.29 us (2%)
    pallas_call x1, Pallas kernels, _scores(): pl.pallas_call(lambda *refs: _kernel((rows_per, tokens, width, tiles, chu...  50.4 us
    pallas_call x1, Pallas kernels, _scores(): pl.pallas_call(lambda *refs: _finish_kernel(tokens, rows_per, *refs), out...  1.12 us

profile of v5, /device:TPU:0, one launch (start us, length us, event | category | flops | bytes accessed | tf_op | source)
XLA Modules:
  0.0 52.8 jit_solution(9078755583140819776)
XLA Ops:
  1.3 50.4 %head.1 = (f32[16,19072]{1,0:T(8,128)S(1)}, f32[8,2,8,128]{3,2,1,0:T(8,128)S(1)}) custom-call(bf16[16,1536]{1,0:T(8,128)(2,1)} %refs_0_.1, bf16[12,128]{1,0:T(8,128)(2,1)} %bitcast.7, bf16[192,151936]{1,0:T(8,128)(2,1)} %bitcast.6, s32[16]{0:T(128)} %refs_3_.1, f32[1]{0:T(128)} %bitcast.5.refs_4_), custom_call_target="tpu_custom_call" | custom-call | tf_op jit(solution)/shard_map/head/pallas_call | solution.py:372
  51.7 1.1 %finish.1 = (bf16[16,18992]{1,0:T(8,128)(2,1)}, f32[1,16]{1,0:T(1,128)}, f32[1,16]{1,0:T(1,128)}) custom-call(f32[16,19072]{1,0:T(8,128)S(1)} %get-tuple-element.8.refs_0_, f32[8,2,8,128]{3,2,1,0:T(8,128)S(1)} %get-tuple-element.9.refs_1_), custom_call_target="tpu_custom_call" | custom-call | tf_op jit(solution)/shard_map/finish/pallas_call | solution.py:399

commit v6 on v5

--- a/solution.py
+++ b/solution.py
@@ -63,7 +63,7 @@
             return table_copy(0, q, (HEAD, MID, head_sem.at[3 + q // 2]))
         return table_copy(0, q, (MID, chunk, tsem.at[q // 2]))
 
-    for n in (0, 1, 2, 3):
+    for n in (0, 1, 2, 3, 4, 5):
         first_copy(n).start()
 
     barrier = pltpu.get_barrier_semaphore()
@@ -71,7 +71,7 @@
         pl.semaphore_signal(barrier, inc=1, device_id={'tp': peer}, device_id_type=MESH)
 
     small[0].wait()
-    for n in (4, 5):
+    for n in (6, 7, 8, 9, 10, 11):
         first_copy(n).start()
     h = hid[...].astype(jnp.float32)
     inv_rms = lax.rsqrt(jnp.mean(h * h, axis=-1, keepdims=True) + NORM_EPS)
@@ -84,8 +84,6 @@
     u = jnp.concatenate([u0, u1], axis=1)
     u = jnp.where(core == 0, u[:, :width], u[:, 2 * LANES - width:])
     normed[...] = u.astype(jnp.bfloat16)
-    for n in (6, 7, 8, 9, 10, 11):
-        first_copy(n).start()
 
     pl.semaphore_wait(barrier, 3)
 
@@ -220,8 +218,20 @@
 
     pieces = [(j, 0, chunk) for j in range(nl - 1)] + [(nl - 1, 0, chunk - LAST), (nl - 1, chunk - LAST, chunk)]
 
+    def first_sent():
+        remote(own.at[pl.ds(0, 2 * nl)], r1, 1, s1_rsem.at[0], xn).wait_send()
+
+    @pl.when(core == 1)
+    def _():
+        first_sent()
+
     for n, (j, lo, hi) in enumerate(pieces):
         i = 2 * nl + j
+        if n in (1, 2):
+            @pl.when(core == 1)
+            def _():
+                pj, plo, phi = pieces[n - 1]
+                stage2_pair(pj, plo, phi, n - 1).wait_send()
         for lane in range(2):
             own[i, lane, :, lo:hi] = own[i, lane, :, lo:hi] + prec[i, lane, :, lo:hi] + r1[j, lane, :, lo:hi]
             stage2(lane, j, lo, hi, n).start()
@@ -304,10 +314,16 @@
         cur = nxt
 
     remote(psend, prec, 0, d2d_rsem.at[0], partner).wait_send()
-    sent1 = own.at[pl.ds(0, 2 * nl)]
-    remote(sent1, r1, 1, s1_rsem.at[0], xn).wait_send()
-    sent2 = own.at[pl.ds(2 * nl, nl)]
-    remote(sent2, r2, 2, s2_rsem.at[0], yn).wait_send()
+    @pl.when(core == 0)
+    def _():
+        first_sent()
+    for n, (j, lo, hi) in enumerate(pieces):
+        if n + 1 in (1, 2):
+            @pl.when(core == 0)
+            def _():
+                stage2_pair(j, lo, hi, n).wait_send()
+        else:
+            stage2_pair(j, lo, hi, n).wait_send()
 
     seven = every.at[pl.ds(0, 7)]
     remote(seven, seven, 3, st_rsem.at[0], partner).wait_recv()

time: 52.9 us -> 52.1 us (0.985)
  Pallas kernels: 51.5 us -> 50.7 us
    pallas_call x1, Pallas kernels: 50.4 us -> 49.6 us  [_scores(): pl.pallas_call(lambda *refs: _kernel((rows_per, tokens, width, tiles, chu...]
where the time goes in v6:
time: 52.1 us; the launch traced here: 52 us
  Pallas kernels  50.7 us (97%)
  between operations  1.29 us (2%)
    pallas_call x1, Pallas kernels, _scores(): pl.pallas_call(lambda *refs: _kernel((rows_per, tokens, width, tiles, chu...  49.6 us
    pallas_call x1, Pallas kernels, _scores(): pl.pallas_call(lambda *refs: _finish_kernel(tokens, rows_per, *refs), out...  1.12 us

profile of v6, /device:TPU:0, one launch (start us, length us, event | category | flops | bytes accessed | tf_op | source)
XLA Modules:
  0.0 52.0 jit_solution(2344784822670113540)
XLA Ops:
  1.3 49.6 %head.1 = (f32[16,19072]{1,0:T(8,128)S(1)}, f32[8,2,8,128]{3,2,1,0:T(8,128)S(1)}) custom-call(bf16[16,1536]{1,0:T(8,128)(2,1)} %refs_0_.1, bf16[12,128]{1,0:T(8,128)(2,1)} %bitcast.7, bf16[192,151936]{1,0:T(8,128)(2,1)} %bitcast.6, s32[16]{0:T(128)} %refs_3_.1, f32[1]{0:T(128)} %bitcast.5.refs_4_), custom_call_target="tpu_custom_call" | custom-call | tf_op jit(solution)/shard_map/head/pallas_call | solution.py:388
  50.9 1.1 %finish.1 = (bf16[16,18992]{1,0:T(8,128)(2,1)}, f32[1,16]{1,0:T(1,128)}, f32[1,16]{1,0:T(1,128)}) custom-call(f32[16,19072]{1,0:T(8,128)S(1)} %get-tuple-element.8.refs_0_, f32[8,2,8,128]{3,2,1,0:T(8,128)S(1)} %get-tuple-element.9.refs_1_), custom_call_target="tpu_custom_call" | custom-call | tf_op jit(solution)/shard_map/finish/pallas_call | solution.py:415

commit v7 on v6

--- a/solution.py
+++ b/solution.py
@@ -8,7 +8,7 @@
 NORM_EPS = 1e-6
 LANES = 128
 LANE_CHUNKS = 3
-DEPTH = 3
+DEPTH = 2
 HEAD, MID = 4 * LANES, 11 * LANES
 LAST = 5 * LANES
 GROUP = 5
@@ -79,11 +79,11 @@
     gain32[...] = gain[...].astype(jnp.float32)
     g0 = (me * 3) // 2
     hc = hid[:, pl.ds(pl.multiple_of(g0 * LANES, LANES), 2 * LANES)].astype(jnp.float32)
-    u0 = hc[:, :LANES] * inv_rms * gain32[pl.ds(g0, 1), :]
-    u1 = hc[:, LANES:] * inv_rms * gain32[pl.ds(g0 + 1, 1), :]
-    u = jnp.concatenate([u0, u1], axis=1)
-    u = jnp.where(core == 0, u[:, :width], u[:, 2 * LANES - width:])
-    normed[...] = u.astype(jnp.bfloat16)
+    gc = jnp.concatenate([gain32[pl.ds(g0, 1), :], gain32[pl.ds(g0 + 1, 1), :]], axis=1)
+
+    def own_cols(v):
+        return jnp.where(core == 0, v[:, :width], v[:, 2 * LANES - width:])
+    normed[...] = (own_cols(hc) * inv_rms * own_cols(gc)).astype(jnp.bfloat16)
 
     pl.semaphore_wait(barrier, 3)
 
@@ -158,13 +158,13 @@
         first_copy(q).wait()
         multiply(0, q, slice(0, HEAD))
         d2d_part(q, 0, HEAD, head_sem.at[5 + q]).start()
-    landed(1, 0, HEAD, head_sem.at[2])
-    for q in range(2, 4):
-        multiply(0, q, slice(0, HEAD))
     landed(0, HEAD, MID, head_sem.at[3])
     for q in range(2):
         multiply(0, q, slice(HEAD, MID))
         d2d_part(q, HEAD, MID, head_sem.at[7]).start()
+    landed(1, 0, HEAD, head_sem.at[2])
+    for q in range(2, 4):
+        multiply(0, q, slice(0, HEAD))
     for q in range(4):
         table_copy(1, q).start()
     for lane in range(2):
@@ -346,7 +346,7 @@
     m_all = tree(jnp.maximum, tops)
     s_all = tree(jnp.add, [blocks_ref[d, 1] * jnp.exp(tops[d] - m_all) for d in range(8)])
     log_all = m_all + jnp.log(s_all)
-    scale = rows16(jnp.exp(blocks_ref[lax.axis_index('tp'), 0] - log_all), 0)
+    scale = rows16(jnp.exp(blocks_ref[lax.axis_index('tp'), 0] - m_all) / s_all, 0)
     log_norm = rows16(log_all, 0)
     p_all = rows16(tree(jnp.add, tops), 64)
 

time: 52.1 us -> 52.1 us (level)
  no operation moved by 1% of the time
where the time goes in v7:
time: 52.1 us; the launch traced here: 52 us
  Pallas kernels  50.7 us (97%)
  between operations  1.29 us (2%)
    pallas_call x1, Pallas kernels, _scores(): pl.pallas_call(lambda *refs: _kernel((rows_per, tokens, width, tiles, chu...  49.6 us
    pallas_call x1, Pallas kernels, _scores(): pl.pallas_call(lambda *refs: _finish_kernel(tokens, rows_per, *refs), out...  1.12 us

profile of v7, /device:TPU:0, one launch (start us, length us, event | category | flops | bytes accessed | tf_op | source)
XLA Modules:
  0.0 52.0 jit_solution(17806925198927393134)
XLA Ops:
  1.3 49.6 %head.1 = (f32[16,19072]{1,0:T(8,128)S(1)}, f32[8,2,8,128]{3,2,1,0:T(8,128)S(1)}) custom-call(bf16[16,1536]{1,0:T(8,128)(2,1)} %refs_0_.1, bf16[12,128]{1,0:T(8,128)(2,1)} %bitcast.7, bf16[192,151936]{1,0:T(8,128)(2,1)} %bitcast.6, s32[16]{0:T(128)} %refs_3_.1, f32[1]{0:T(128)} %bitcast.5.refs_4_), custom_call_target="tpu_custom_call" | custom-call | tf_op jit(solution)/shard_map/head/pallas_call | solution.py:388
  50.8 1.1 %finish.1 = (bf16[16,18992]{1,0:T(8,128)(2,1)}, f32[1,16]{1,0:T(1,128)}, f32[1,16]{1,0:T(1,128)}) custom-call(f32[16,19072]{1,0:T(8,128)S(1)} %get-tuple-element.8.refs_0_, f32[8,2,8,128]{3,2,1,0:T(8,128)S(1)} %get-tuple-element.9.refs_1_), custom_call_target="tpu_custom_call" | custom-call | tf_op jit(solution)/shard_map/finish/pallas_call | solution.py:415

commit v8 on v7

--- a/solution.py
+++ b/solution.py
@@ -157,20 +157,17 @@
     for q in range(2):
         first_copy(q).wait()
         multiply(0, q, slice(0, HEAD))
-        d2d_part(q, 0, HEAD, head_sem.at[5 + q]).start()
+        d2d_part(q, 0, HEAD, head_sem.at[5]).start()
     landed(0, HEAD, MID, head_sem.at[3])
     for q in range(2):
         multiply(0, q, slice(HEAD, MID))
-        d2d_part(q, HEAD, MID, head_sem.at[7]).start()
+        d2d_part(q, HEAD, MID, head_sem.at[6]).start()
     landed(1, 0, HEAD, head_sem.at[2])
     for q in range(2, 4):
         multiply(0, q, slice(0, HEAD))
     for q in range(4):
         table_copy(1, q).start()
-    for lane in range(2):
-        d2d_part(lane, 0, HEAD, head_sem.at[5 + lane]).wait_recv()
-        own[0, lane, :, :HEAD] = own[0, lane, :, :HEAD] + prec[0, lane, :, :HEAD]
-        stage1_part(lane, 0, HEAD).start()
+    head_pair(0, HEAD, head_sem.at[5])
     landed(0, MID, chunk, tsem.at[0])
     for q in range(2):
         multiply(0, q, slice(MID, chunk))
@@ -178,7 +175,7 @@
     landed(1, HEAD, MID, head_sem.at[4])
     for q in range(2, 4):
         multiply(0, q, slice(HEAD, MID))
-    head_pair(HEAD, MID, head_sem.at[7])
+    head_pair(HEAD, MID, head_sem.at[6])
     for i in range(2, DEPTH):
         for q in range(4):
             table_copy(i, q).start()
@@ -405,7 +402,7 @@
             pltpu.VMEM((tokens, tiles * LANES), f32),
             pltpu.VMEM((2, tokens // 2, LANES), f32),
             pltpu.VMEM((8, 2, tokens // 2, LANES), f32),
-            dma((3,)), dma((DEPTH * 2,)), dma((8,)),
+            dma((3,)), dma((DEPTH * 2,)), dma((7,)),
             dma((2 * nl + 1,)), dma((2,)), dma((nl + 1,)), dma((1,)), dma((4,)),
         ],
         compiler_params=pltpu.CompilerParams(collective_id=0, has_side_effects=True,

time: 52.1 us -> 52.1 us (level)
  no operation moved by 1% of the time
where the time goes in v8:
time: 52.1 us; the launch traced here: 52 us
  Pallas kernels  50.7 us (97%)
  between operations  1.29 us (2%)
    pallas_call x1, Pallas kernels, _scores(): pl.pallas_call(lambda *refs: _kernel((rows_per, tokens, width, tiles, chu...  49.6 us
    pallas_call x1, Pallas kernels, _scores(): pl.pallas_call(lambda *refs: _finish_kernel(tokens, rows_per, *refs), out...  1.12 us

profile of v8, /device:TPU:0, one launch (start us, length us, event | category | flops | bytes accessed | tf_op | source)
XLA Modules:
  0.0 52.0 jit_solution(2454257269920575693)
XLA Ops:
  1.3 49.6 %head.1 = (f32[16,19072]{1,0:T(8,128)S(1)}, f32[8,2,8,128]{3,2,1,0:T(8,128)S(1)}) custom-call(bf16[16,1536]{1,0:T(8,128)(2,1)} %refs_0_.1, bf16[12,128]{1,0:T(8,128)(2,1)} %bitcast.7, bf16[192,151936]{1,0:T(8,128)(2,1)} %bitcast.6, s32[16]{0:T(128)} %refs_3_.1, f32[1]{0:T(128)} %bitcast.5.refs_4_), custom_call_target="tpu_custom_call" | custom-call | tf_op jit(solution)/shard_map/head/pallas_call | solution.py:385
  50.8 1.1 %finish.1 = (bf16[16,18992]{1,0:T(8,128)(2,1)}, f32[1,16]{1,0:T(1,128)}, f32[1,16]{1,0:T(1,128)}) custom-call(f32[16,19072]{1,0:T(8,128)S(1)} %get-tuple-element.8.refs_0_, f32[8,2,8,128]{3,2,1,0:T(8,128)S(1)} %get-tuple-element.9.refs_1_), custom_call_target="tpu_custom_call" | custom-call | tf_op jit(solution)/shard_map/finish/pallas_call | solution.py:412
